TPU v7x, 32 devices: a whole 2x2x4 slice. The times are simulated.
32 devices in a mesh: lat: 2 (over y), lon: 8 (over z, core), freq: 2 (over x).
Axes of the slice: x: 2, y: 2, z: 4, core: 2. Of those that a mesh axis runs over, the one named last changes fastest.
Arguments:
- spectrum: float32 [36, 36, 8, 1024], P('freq', None, 'lat', 'lon'), may hold values from 0.05 to 1
- group_speed: float32 [36], P('freq'), may hold values from 0.15 to 0.6
- sea_mask: int32 [8, 1024], P('lat', 'lon'), may hold values 0 or 1
- wind_growth: float32 [8, 1024], P('lat', 'lon'), may hold values from 0.2 to 2
- dissipation: float32 [8, 1024], P('lat', 'lon'), may hold values from 0.1 to 1
- wind_profile: float32 [1296], replicated, may hold values from 0.02 to 0.2
- nonlinear_coef: float32 [1296], replicated, may hold values from 0.05 to 0.5
- momentum: float32 [2, 1296], replicated, may hold values from -6 to 6
- quadruplet: int32 [2, 1296], replicated, may hold values from 0 to 1295, as said below
- ocean_cell: int32 [8, 1024], P('lat', 'lon'), may hold values from 0 to 8191, as said below
Outputs:
- spectrum_out: float32 [36, 36, 8, 1024], P('freq', None, 'lat', 'lon')
- ocean_stress: float32 [8192, 2], P(('lon', 'freq'))
Inputs may be any that keep to these rules, and one draw needn't show every extreme that they name: quadruplet[0, b] names a bin 1 or 2 frequencies higher (at most the highest) and 1 to 6 directions further, cyclically; quadruplet[1, b] one 1 or 2 frequencies lower (at least the lowest) and 1 to 6 directions back. ocean_cell[i, j] = j * 8 + i2 with i2 within 1 of i.
All inputs are finite; a program needn't handle non-finite values. No bound on the sum of `sea_mask` on one device may be relied on, other than what follows from the above.
Results may differ from a plain program's by a relative error of at most 0.000094.
Values sent between devices are 32-bit elements; how exact they have to be, the bound alone decides.
A program may use at most 64 MiB of HBM per device.

v0:
```python
import functools

import jax
import jax.numpy as jnp
import numpy as np
from jax import lax
from jax.experimental import pallas as pl
from jax.experimental.pallas import tpu as pltpu
from jax.sharding import PartitionSpec as P

time_step = 0.5
MESH = pl.DeviceIdType.MESH
VMEM = pltpu.VMEM


def spread(nf):
    order = list(range(4)) + list(range(nf - 4, nf)) + list(range(4, nf - 4))
    return {f: i for i, f in enumerate(order)}


def propagate_kernel(
    sizes, spectrum, *refs
):
    sources, refs = refs[:10], refs[10:]
    result, stress, *refs = refs
    inputs, refs = refs[:10], refs[10:]
    speed, waves, profile, coef, momentum, quad, mask, wind, dissip, cells = inputs
    (
        x, moved, trans, table, rates, cols, lines, pack_up, pack_down, got_up, got_down,
        edge_rows, lon_pack, got_left, got_right, part, parts,
        load_sem, small_sem, lat_send, lat_recv, lon_send, lon_recv, freq_send, freq_recv,
        part_send, part_recv,
    ) = refs
    n_lat, n_lon, n_freq, nf, nd, rows, nbins = sizes
    half = nd // 2
    pair = 2 * nd
    margin = 4 * nd
    band = nf * nd
    places = spread(nf)
    li, lo, fi = lax.axis_index("lat"), lax.axis_index("lon"), lax.axis_index("freq")
    load = pltpu.make_async_copy(spectrum, x, load_sem)
    load.start()
    small = [
        pltpu.make_async_copy(a, b, small_sem.at[i])
        for i, (a, b) in enumerate(zip(sources, inputs))
    ]
    for copy in small:
        copy.start()

    east, west = lax.rem(lo + 1, n_lon), lax.rem(lo + n_lon - 1, n_lon)
    group = []
    for s in range(1, n_lat * n_freq):
        dl, df = divmod(s, n_freq)
        group.append(
            (dl, {"lat": lax.rem(li + dl, n_lat), "freq": lax.rem(fi + df, n_freq)})
        )
    barrier = pltpu.get_barrier_semaphore()
    for peer in [{"lon": east}, {"lon": west}] + [g for _, g in group]:
        pl.semaphore_signal(barrier, inc=1, device_id=peer, device_id_type=MESH)

    total_rows = pack_up.shape[0]
    pieces = ((0, 4 * half), (4 * half, 4 * half), (8 * half, total_rows - 8 * half))

    def lat_copy(k, up):
        if isinstance(k, int):
            at, size = pieces[k]
        else:
            at, size = pl.multiple_of(k * (4 * half), 8), 4 * half
        src, dst = (pack_up, got_up) if up else (pack_down, got_down)
        i = k if up else 3 + k
        return pltpu.make_async_remote_copy(
            src.at[pl.ds(at, size)], dst.at[pl.ds(at, size)],
            lat_send.at[i], lat_recv.at[i],
            device_id={"lat": li + 1 if up else li - 1}, device_id_type=MESH,
        )

    def freq_copy(up):
        src = band if up else margin
        dst = 0 if up else margin + band
        return pltpu.make_async_remote_copy(
            moved.at[pl.ds(src, margin)], moved.at[pl.ds(dst, margin)],
            freq_send.at[int(up)], freq_recv.at[int(up)],
            device_id={"freq": fi + 1 if up else fi - 1}, device_id_type=MESH,
        )

    def lon_copy(to_east):
        return pltpu.make_async_remote_copy(
            lon_pack, got_left if to_east else got_right,
            lon_send.at[int(to_east)], lon_recv.at[int(to_east)],
            device_id={"lon": east if to_east else west}, device_id_type=MESH,
        )

    def part_copy(s):
        return pltpu.make_async_remote_copy(
            part, parts.at[s], part_send.at[s], part_recv.at[s],
            device_id=group[s][1], device_id_type=MESH,
        )

    up_ok, down_ok = li < n_lat - 1, li > 0
    near = lax.div(n_freq - fi, n_freq)
    order = (near, 1 - near, 2)

    for copy in small:
        copy.wait()
    span = lines.shape[1]
    rates[...] = jnp.zeros_like(rates)
    rates[0:1, 0:nf] = speed[...].reshape(1, nf)
    lines[...] = jnp.zeros_like(lines)
    lines[0:2, 0:nbins] = (quad[...] - (fi * band - margin)).astype(jnp.float32)
    lines[2:3, 0:nbins] = coef[...].reshape(1, nbins)
    weight = profile[...].reshape(1, nbins)
    lines[3:4, 0:nbins] = weight
    lines[4:6, 0:nbins] = momentum[...] * weight
    lines[...] = pltpu.roll(lines[...], lax.rem(margin - fi * band + span, span), 1)
    for k in range(cols.shape[0] // 128):
        cols[pl.ds(128 * k, 128), :] = lines[:, 128 * k : 128 * k + 128].T
    turned = waves[...].T
    table[pl.ds(0, pair), :] = jnp.broadcast_to(turned[0:pair, 0:1], (pair, 128))
    table[pl.ds(pair, pair), :] = jnp.broadcast_to(turned[0:pair, 1:2], (pair, 128))

    pack_up[pl.ds(total_rows - 8, 8), :] = jnp.zeros((8, 128), jnp.float32)
    pack_down[pl.ds(total_rows - 8, 8), :] = jnp.zeros((8, 128), jnp.float32)
    load.wait()
    for f in range(nf):
        at = half * places[f]
        pack_up[pl.ds(at, half), :] = x[pl.ds(nd * f * rows + rows - 1, half, stride=rows), :]
        pack_down[pl.ds(at, half), :] = x[pl.ds((nd * f + half) * rows, half, stride=rows), :]

    lane = lax.broadcasted_iota(jnp.int32, (pair, 128), 1)
    row = lax.broadcasted_iota(jnp.int32, (pair, 128), 0)
    row = jnp.where(row >= nd, row - nd, row)
    low = row < half
    forward = table[pl.ds(0, pair), :] > 0.0
    rim = lane == jnp.where(forward, 0, 127)
    sent = lane == jnp.where(forward, 127, 0)

    def shifted(e):
        return jnp.where(forward, pltpu.roll(e, 1, 1), pltpu.roll(e, 127, 1))

    def load_row(c, r):
        return x[pl.ds(pair * rows * c + r, pair, stride=rows), :]

    def pack_step(c, acc):
        for r in range(rows):
            z = jnp.where(sent, load_row(c, r), 0.0)
            acc = acc + pltpu.roll(z, c * rows + r, 1)
        return acc

    lon_pack[...] = lax.fori_loop(0, nf // 2, pack_step, jnp.zeros((pair, 128), jnp.float32))
    pl.semaphore_wait(barrier, 2 + len(group))

    @pl.when(up_ok)
    def _():
        for k in order:
            lat_copy(k, True).start()

    @pl.when(down_ok)
    def _():
        for k in order:
            lat_copy(k, False).start()

    lon_copy(True).start()
    lon_copy(False).start()

    @pl.when(jnp.logical_not(down_ok))
    def _():
        got_up[...] = jnp.zeros_like(got_up)

    @pl.when(jnp.logical_not(up_ok))
    def _():
        got_down[...] = jnp.zeros_like(got_down)

    @pl.when(fi == 0)
    def _():
        moved[pl.ds(0, margin), :] = jnp.zeros((margin, rows * 128), jnp.float32)

    @pl.when(fi == n_freq - 1)
    def _():
        moved[pl.ds(margin + band, margin), :] = jnp.zeros((margin, rows * 128), jnp.float32)

    def receive(k, first, count):
        @pl.when(down_ok)
        def _():
            lat_copy(k, True).wait_recv()

        @pl.when(up_ok)
        def _():
            lat_copy(k, False).wait_recv()

        base = pieces[2][0] if isinstance(k, int) else pl.multiple_of(k * (4 * half), 8)
        for j in range(count):
            f, at = first + j, base + half * j
            edge_rows[pl.ds(nd * f, half), :] = got_up[pl.ds(at, half), :]
            edge_rows[pl.ds(nd * f + half, half), :] = got_down[pl.ds(at, half), :]

    def chunk(c, sums):
        rate = pltpu.roll(rates[...], 128 - 2 * c, 1)
        g = jnp.where(
            lax.broadcasted_iota(jnp.int32, (pair, 128), 0) < nd,
            jnp.broadcast_to(rate[0:1, 0:1], (pair, 128)),
            jnp.broadcast_to(rate[0:1, 1:2], (pair, 128)),
        )
        ax = g * jnp.abs(table[pl.ds(0, pair), :])
        ay = g * jnp.abs(table[pl.ds(pair, pair), :])
        halo = got_left[...]
        at = pl.multiple_of(pair * c, 8)
        outer = edge_rows[pl.ds(at, pair), :]
        here = pl.multiple_of(margin + pair * c, 8)
        w0 = cols[pl.ds(here, pair), 4:5]
        w1 = cols[pl.ds(here, pair), 5:6]
        e = [load_row(c, r) for r in range(rows)]
        out = []
        for r in range(rows):
            k = c * rows + r
            nx = jnp.where(rim, pltpu.roll(halo, 128 - k, 1), shifted(e[r]))
            below = e[r - 1] if r > 0 else outer
            above = e[r + 1] if r < rows - 1 else outer
            ny = jnp.where(low, below, above)
            m = (e[r] - ax * (e[r] - nx) - ay * (e[r] - ny)) * mask[r : r + 1, :].astype(jnp.float32)
            moved[pl.ds(here, pair), r * 128 : (r + 1) * 128] = m
            for i, v in enumerate((m, m * w0, m * w1)):
                s = sums[3 * r + i]
                for j in range(pair // 8):
                    s = s + v[8 * j : 8 * j + 8]
                out.append(s)
        return tuple(out)

    sums = tuple(jnp.zeros((8, 128), jnp.float32) for _ in range(3 * rows))
    lon_copy(True).wait_recv()
    lon_copy(False).wait_recv()
    got_left[...] = jnp.where(
        forward, pltpu.roll(got_left[...], 1, 1), pltpu.roll(got_right[...], 127, 1)
    )
    for k in (near, 1 - near):
        receive(k, k * (nf - 4), 4)
        sums = lax.fori_loop(k * (nf // 2 - 2), k * (nf // 2 - 2) + 2, chunk, sums)

        @pl.when(jnp.logical_and(k == 0, fi > 0))
        def _():
            freq_copy(False).start()

        @pl.when(jnp.logical_and(k == 1, fi < n_freq - 1))
        def _():
            freq_copy(True).start()

    receive(2, 4, nf - 8)
    sums = lax.fori_loop(2, nf // 2 - 2, chunk, sums)

    all_rows = n_lat * rows
    part[pl.ds(0, 8), :] = jnp.zeros((8, 128), jnp.float32)
    ids = (lo * 128 + lax.broadcasted_iota(jnp.int32, (all_rows, 128), 1)) * all_rows
    ids = ids + lax.broadcasted_iota(jnp.int32, (all_rows, 128), 0)
    totals = [jnp.zeros((all_rows, 128), jnp.float32) for _ in range(2)]
    for r in range(rows):
        part[r : r + 1, :] = jnp.sum(sums[3 * r], axis=0, keepdims=True)
        hit = cells[r : r + 1, :] == ids
        for i in range(2):
            tau = wind[r : r + 1, :] * jnp.sum(sums[3 * r + 1 + i], axis=0, keepdims=True)
            totals[i] = totals[i] + jnp.where(hit, tau, 0.0)
    for i in range(2):
        part[pl.ds(8 + i * all_rows, all_rows), :] = totals[i]
    for s in range(len(group)):
        part_copy(s).start()

    chunks = nf // 2 + 4
    is_low, is_high = fi == 0, fi == n_freq - 1
    t_from = jnp.where(is_low, 1, 3)
    t_to = jnp.where(is_high, chunks - 1, chunks - 3)
    o_from = jnp.where(is_low, 2, 4)
    o_to = jnp.where(is_high, chunks - 2, chunks - 4)
    lane3 = lax.broadcasted_iota(jnp.int32, (pair, 3 * pair), 1)
    row3 = lax.broadcasted_iota(jnp.int32, (pair, 3 * pair), 0)

    def interact(c, carry):
        at = pl.multiple_of(pair * c, 8)
        prior = pl.multiple_of(pair * c - pair, 8)
        where = (lane3 + prior).astype(jnp.float32)
        picks = [
            jnp.where(cols[pl.ds(at, pair), i : i + 1] == where, 1.0, 0.0).astype(jnp.bfloat16)
            for i in range(2)
        ]
        both = select_dot(jnp.concatenate(picks, axis=0), moved[pl.ds(prior, 3 * pair), :])
        third, fourth = both[:pair], both[pair:]
        e = moved[pl.ds(at, pair), :]
        trans[pl.ds(at, pair), :] = cols[pl.ds(at, pair), 2:3] * (
            e * e * (third + fourth) - 2.0 * e * third * fourth
        )
        return carry

    def finish(c, carry):
        at = pl.multiple_of(pair * c, 8)
        prior = pl.multiple_of(pair * c - pair, 8)
        own_bin = (row3 + at).astype(jnp.float32)
        line = pltpu.roll(lines[...], span - prior, 1)
        put = jnp.where(line[0:1, : 3 * pair] == own_bin, 1.0, 0.0) + jnp.where(
            line[1:2, : 3 * pair] == own_bin, 1.0, 0.0
        )
        back = select_dot(put.astype(jnp.bfloat16), trans[pl.ds(prior, 3 * pair), :])
        back = back - 2.0 * trans[pl.ds(at, pair), :]
        shape = cols[pl.ds(at, pair), 3:4]
        for r in range(rows):
            here = slice(r * 128, (r + 1) * 128)
            e = moved[pl.ds(at, pair), here]
            loss = dissip[r : r + 1, :] * total_energy[r : r + 1, :]
            tendency = wind[r : r + 1, :] * shape * e + back[:, here] - loss * e
            result[pl.ds(rows * pair * (c - 2) + r, pair, stride=rows), :] = mask[
                r : r + 1, :
            ].astype(jnp.float32) * (e + time_step * tendency)
        return carry

    lax.fori_loop(t_from, t_to, interact, 0)
    for s in range(len(group)):
        part_copy(s).wait()
    en = part[pl.ds(0, 8), :]
    st = part[pl.ds(8, 2 * all_rows), :]
    for s, (dl, _) in enumerate(group):
        if dl == 0:
            en = en + parts[s, pl.ds(0, 8), :]
        st = st + parts[s, pl.ds(8, 2 * all_rows), :]
    total_energy = en / nbins
    share = (128 // n_freq) * all_rows
    cell = lax.broadcasted_iota(jnp.int32, (128, share), 1)
    first_cell = (lax.broadcasted_iota(jnp.int32, (128, share), 0) - fi * (128 // n_freq)) * all_rows
    inside = jnp.logical_and(cell >= first_cell, cell < first_cell + all_rows)
    wide = jnp.dot(
        st, jnp.where(inside, 1.0, 0.0),
        precision=lax.Precision.HIGHEST, preferred_element_type=jnp.float32,
    )
    place = lax.broadcasted_iota(jnp.int32, (all_rows, share), 1) & (all_rows - 1)
    own_row = place == lax.broadcasted_iota(jnp.int32, (all_rows, share), 0)
    for i in range(2):
        picked = jnp.where(own_row, wide[i * all_rows : (i + 1) * all_rows], 0.0)
        stress[i : i + 1, :] = jnp.sum(picked, axis=0, keepdims=True)
    lax.fori_loop(o_from, o_to, finish, 0)

    @pl.when(fi > 0)
    def _():
        freq_copy(True).wait_recv()

    @pl.when(fi < n_freq - 1)
    def _():
        freq_copy(False).wait_recv()

    lax.fori_loop(1, t_from, interact, 0)
    lax.fori_loop(t_to, chunks - 1, interact, 0)
    lax.fori_loop(2, o_from, finish, 0)
    lax.fori_loop(o_to, chunks - 2, finish, 0)

    lon_copy(True).wait_send()
    lon_copy(False).wait_send()

    @pl.when(up_ok)
    def _():
        for k in range(3):
            lat_copy(k, True).wait_send()

    @pl.when(down_ok)
    def _():
        for k in range(3):
            lat_copy(k, False).wait_send()

    @pl.when(fi > 0)
    def _():
        freq_copy(False).wait_send()

    @pl.when(fi < n_freq - 1)
    def _():
        freq_copy(True).wait_send()

def split(v):
    high = v.astype(jnp.bfloat16)
    return high, (v - high.astype(jnp.float32)).astype(jnp.bfloat16)


def select_dot(pick, window):
    high, low = split(window)
    return jnp.dot(pick, high, preferred_element_type=jnp.float32) + jnp.dot(
        pick, low, preferred_element_type=jnp.float32
    )


def local(
    axes,
    spectrum,
    group_speed,
    sea_mask,
    wind_growth,
    dissipation,
    wind_profile,
    nonlinear_coef,
    momentum,
    quadruplet,
    ocean_cell,
):
    n_lat, n_lon, n_freq = axes
    nf, nd, rows, width = spectrum.shape
    nbins = wind_profile.shape[0]
    band, margin, pair, half = nf * nd, 4 * nd, 2 * nd, nd // 2
    ext = band + 2 * margin
    all_rows = n_lat * rows
    f32 = jnp.float32
    angles = (np.float32(2.0 * np.pi) * np.arange(nd, dtype=np.float32) / np.float32(nd)).astype(
        np.float32
    )
    waves = np.zeros((8, 128), np.float32)
    waves[0, :pair], waves[1, :pair] = np.tile(np.cos(angles), 2), np.tile(np.sin(angles), 2)

    packed = -(-nf * half // 8) * 8
    peers = n_lat * n_freq - 1
    small = 8 + 2 * all_rows
    share = (width // n_freq) * all_rows
    span = -(-(nbins + margin) // 128) * 128
    vmem = pl.BlockSpec(memory_space=VMEM)
    sizes = (n_lat, n_lon, n_freq, nf, nd, rows, nbins)
    dma = pltpu.SemaphoreType.DMA
    smalls = (
        group_speed,
        jnp.asarray(waves),
        wind_profile,
        nonlinear_coef,
        momentum,
        quadruplet,
        sea_mask,
        wind_growth,
        dissipation,
        ocean_cell,
    )
    out, ocean = pl.pallas_call(
        functools.partial(propagate_kernel, sizes),
        out_shape=(
            jax.ShapeDtypeStruct((band * rows, width), f32),
            jax.ShapeDtypeStruct((2, share), f32),
        ),
        in_specs=[pl.BlockSpec(memory_space=pltpu.HBM)] * 11,
        out_specs=(vmem, vmem),
        scratch_shapes=[VMEM(a.shape, a.dtype) for a in smalls]
        + [
            VMEM((band * rows, width), f32),
            VMEM((ext, rows * width), f32),
            VMEM((ext, rows * width), f32),
            VMEM((2 * pair, width), f32),
            VMEM((8, width), f32),
            VMEM((-(-ext // 128) * 128, 8), f32),
            VMEM((8, span), f32),
            VMEM((packed, width), f32),
            VMEM((packed, width), f32),
            VMEM((packed, width), f32),
            VMEM((packed, width), f32),
            VMEM((band, width), f32),
            VMEM((pair, width), f32),
            VMEM((pair, width), f32),
            VMEM((pair, width), f32),
            VMEM((small, width), f32),
            VMEM((peers, small, width), f32),
            dma, dma((len(smalls),)),
            dma((6,)), dma((6,)), dma((2,)), dma((2,)), dma((2,)), dma((2,)),
            dma((peers,)), dma((peers,)),
        ],
        compiler_params=pltpu.CompilerParams(
            collective_id=0, has_side_effects=True, vmem_limit_bytes=24 << 20
        ),
    )(
        *[
            pltpu.with_memory_space_constraint(a, pltpu.HBM)
            for a in (spectrum.reshape(band * rows, width), *smalls)
        ]
    )
    return out.reshape(spectrum.shape), ocean.T


def solution(mesh):
    axes = tuple(mesh.shape[a] for a in ("lat", "lon", "freq"))
    return jax.shard_map(
        functools.partial(local, axes),
        mesh=mesh,
        in_specs=(
            P("freq", None, "lat", "lon"),
            P("freq"),
            P("lat", "lon"),
            P("lat", "lon"),
            P("lat", "lon"),
            P(),
            P(),
            P(),
            P(),
            P("lat", "lon"),
        ),
        out_specs=(P("freq", None, "lat", "lon"), P(("lon", "freq"), None)),
        check_vma=False,
    )
```

profile of v0, /device:TPU:0, one launch (start us, length us, event | category | flops | bytes accessed | tf_op | source)
XLA Modules:
  0.0 24.6 jit_solution(4959642841825039462)
XLA Ops:
  0.6 22.3 %shard_map.122 = (f32[2592,128]{1,0:T(8,128)S(1)}, f32[2,512]{1,0:T(2,128)S(1)}) custom-call(f32[2592,128]{1,0:T(8,128)} %bitcast.5, f32[18]{0:T(128)} %refs_0_.1, f32[8,128]{1,0:T(8,128)} %constant.2.clone.refs_1_, f32[1296]{0:T(1024)} %refs_2_.1, f32[1296]{0:T(1024)} %refs_3_.1, f32[2,1296]{1,0:T(2,128)} %refs_4_.1, s32[2,1296]{1,0:T(2,128)} %refs_5_.1, ...), custom_call_target="tpu_custom_call" | custom-call | tf_op jit(solution)/shard_map/pallas_call | solution.py:428
  23.0 1.1 %copy.15 = f32[18,36,4,128]{3,2,1,0:T(4,128)} copy(f32[18,36,4,128]{3,2,1,0:T(4,128)S(1)} %bitcast.3) | data formatting | bytes 2654208
  24.0 0.6 %copy.16 = f32[512,2]{0,1:T(2,128)} copy(f32[512,2]{0,1:T(2,128)S(1)} %bitcast.4) | data formatting | bytes 8192
where the time goes:
time: 24.8 us; the launch traced here: 24.6 us
  Pallas kernels  22.3 us (90%)
  local copies, waits for them, and re-layouts  1.66 us (7%)
  between operations  0.64 us (3%)
    pallas_call x1, Pallas kernels, local(): pl.pallas_call(functools.partial(propagate_kernel, sizes), out_shape=(jax...  22.3 us
    unnamed x2, local copies, waits for them, and re-layouts  1.66 us

commit v1 on v0

v1 whole, which is shorter than its diff:
```python
import functools

import jax
import jax.numpy as jnp
import numpy as np
from jax import lax
from jax.experimental import pallas as pl
from jax.experimental.pallas import tpu as pltpu
from jax.sharding import PartitionSpec as P

time_step = 0.5
MESH = pl.DeviceIdType.MESH
VMEM = pltpu.VMEM
LANES = 128
EDGE = 4
F32, BF16 = jnp.float32, jnp.bfloat16


def spread(nf):
    order = list(range(EDGE)) + list(range(nf - EDGE, nf)) + list(range(EDGE, nf - EDGE))
    return {f: i for i, f in enumerate(order)}


def round_up(n, m):
    return -(-n // m) * m


def split(v):
    high = v.astype(BF16)
    return high, (v - high.astype(F32)).astype(BF16)


def wave_kernel(sizes, angles, spectrum, *refs):
    sources, refs = refs[:10], refs[10:]
    result, stress, *refs = refs
    inputs, refs = refs[:10], refs[10:]
    speed, waves, profile, coef, momentum, quad, mask, wind, dissip, cells = inputs
    (
        x, mf, mh, ml, th, tl, pick, put, table, rates, cols, lines, coefs, shapes, weight0, weight1,
        gains, gains_far, speed_far, pack_up, pack_down, got_up, got_down, edge, edge_far,
        lon_pack, got_left, got_right, lon_far, far_left, far_right, cols_far, part, parts,
        load_sem, small_sem, raw_send, raw_recv, lat_send, lat_recv, lon_send, lon_recv,
        part_send, part_recv,
    ) = refs
    n_lat, n_lon, n_freq, nf, nd, rows, nbins = sizes
    half = nd // 2
    pair = 2 * nd
    band = nf * nd
    pitch = round_up(pair, 16)
    pad = pitch - pair
    own_chunks = nf // 2
    far_chunks = EDGE // 2
    chunks = own_chunks + far_chunks
    window = 3 * pitch
    reach = round_up(window, LANES)
    span = lines.shape[1]
    places = spread(nf)
    groups = pair // 8
    cosines, sines = angles
    li, lo, fi = lax.axis_index("lat"), lax.axis_index("lon"), lax.axis_index("freq")
    other = 1 - fi
    first = far_chunks * fi
    far_first = own_chunks * other

    own_rows = pl.multiple_of(first * (pair * rows), 8)
    load = pltpu.make_async_copy(spectrum, x.at[pl.ds(own_rows, band * rows)], load_sem)
    load.start()
    small = [
        pltpu.make_async_copy(a, b, small_sem.at[i])
        for i, (a, b) in enumerate(zip(sources, inputs))
    ]
    for copy in small:
        copy.start()

    east, west = lax.rem(lo + 1, n_lon), lax.rem(lo + n_lon - 1, n_lon)
    group = []
    for s in range(1, n_lat * n_freq):
        dl, df = divmod(s, n_freq)
        group.append(
            (dl, {"lat": lax.rem(li + dl, n_lat), "freq": lax.rem(fi + df, n_freq)})
        )
    barrier = pltpu.get_barrier_semaphore()
    peers = [{"lon": east}, {"lon": west}]
    peers += [{"lon": east, "freq": other}, {"lon": west, "freq": other}]
    peers += [g for _, g in group]
    for peer in peers:
        pl.semaphore_signal(barrier, inc=1, device_id=peer, device_id_type=MESH)

    packed = pack_up.shape[0]
    far_lat = EDGE * half
    up_ok, down_ok = li < n_lat - 1, li > 0

    def raw_copy():
        count = EDGE * nd * rows
        src = pl.multiple_of(other * ((nf - EDGE) * nd * rows), 8)
        dst = pl.multiple_of(fi * (band * rows), 8)
        return pltpu.make_async_remote_copy(
            spectrum.at[pl.ds(src, count)], x.at[pl.ds(dst, count)],
            raw_send.at[0], raw_recv.at[0], device_id={"freq": other}, device_id_type=MESH,
        )

    def speed_copy():
        return pltpu.make_async_remote_copy(
            sources[0], speed_far, raw_send.at[1], raw_recv.at[1],
            device_id={"freq": other}, device_id_type=MESH,
        )

    def lat_copy(up):
        src, dst = (pack_up, got_up) if up else (pack_down, got_down)
        i = int(up)
        return pltpu.make_async_remote_copy(
            src, dst.at[pl.ds(far_lat, packed)], lat_send.at[i], lat_recv.at[i],
            device_id={"lat": li + 1 if up else li - 1}, device_id_type=MESH,
        )

    def lat_far_copy(up):
        src, dst = (pack_up, got_up) if up else (pack_down, got_down)
        i = 2 + int(up)
        return pltpu.make_async_remote_copy(
            src.at[pl.ds(pl.multiple_of(other * far_lat, 8), far_lat)], dst.at[pl.ds(0, far_lat)],
            lat_send.at[i], lat_recv.at[i],
            device_id={"lat": li + 1 if up else li - 1, "freq": other}, device_id_type=MESH,
        )

    def lon_copy(to_east):
        i = int(to_east)
        return pltpu.make_async_remote_copy(
            lon_pack, got_left if to_east else got_right, lon_send.at[i], lon_recv.at[i],
            device_id={"lon": east if to_east else west}, device_id_type=MESH,
        )

    def lon_far_copy(to_east):
        i = 2 + int(to_east)
        return pltpu.make_async_remote_copy(
            lon_far, far_left if to_east else far_right, lon_send.at[i], lon_recv.at[i],
            device_id={"lon": east if to_east else west, "freq": other}, device_id_type=MESH,
        )

    def part_copy(s):
        return pltpu.make_async_remote_copy(
            part, parts.at[s], part_send.at[s], part_recv.at[s],
            device_id=group[s][1], device_id_type=MESH,
        )

    def signs(values, j):
        return [bool(values[(8 * j + i) % nd] > 0.0) for i in range(8)]

    eight = lax.broadcasted_iota(jnp.int32, (8, LANES), 0)
    lane = lax.broadcasted_iota(jnp.int32, (8, LANES), 1)

    def rows_of(flags):
        spot = None
        for i, flag in enumerate(flags):
            if flag:
                here = eight == i
                spot = here if spot is None else jnp.logical_or(spot, here)
        return spot

    def choose(flags, yes, no):
        if all(flags):
            return yes()
        if not any(flags):
            return no()
        return jnp.where(rows_of(flags), yes(), no())

    forward = [signs(cosines, j) for j in range(groups)]
    southern = [[(8 * j + i) % nd < half for i in range(8)] for j in range(groups)]

    pack_up[pl.ds(packed - 8, 8), :] = jnp.zeros((8, LANES), F32)
    pack_down[pl.ds(packed - 8, 8), :] = jnp.zeros((8, LANES), F32)
    load.wait()
    for f in range(nf):
        at = half * places[f]
        base = own_rows + nd * f * rows
        pack_up[pl.ds(at, half), :] = x[pl.ds(base + rows - 1, half, stride=rows), :]
        pack_down[pl.ds(at, half), :] = x[pl.ds(base + half * rows, half, stride=rows), :]

    step = 3 if own_chunks % 3 == 0 else 1

    def pack_step(t, acc):
        acc = list(acc)
        for u in range(step):
            c = t * step + u + first
            base = pl.multiple_of(c * (pair * rows), 8)
            for r in range(rows):
                k = c * rows + r
                for j in range(groups):
                    e = x[pl.ds(base + 8 * rows * j + r, 8, stride=rows), :]
                    z = choose(
                        forward[j],
                        lambda: jnp.where(lane == LANES - 1, e, 0.0),
                        lambda: jnp.where(lane == 0, e, 0.0),
                    )
                    acc[j] = acc[j] + pltpu.roll(z, k, 1)
        return tuple(acc)

    sums = lax.fori_loop(
        0, own_chunks // step, pack_step, tuple(jnp.zeros((8, LANES), F32) for _ in range(groups))
    )
    for j in range(groups):
        aligned = choose(forward[j], lambda: pltpu.roll(sums[j], 1, 1), lambda: sums[j])
        lon_pack[8 * j : 8 * j + 8, :] = aligned
    begin = (first + (own_chunks - far_chunks) * other) * rows
    whole = jnp.concatenate(
        [lon_pack[...], jnp.zeros((LANES - pair, LANES), F32)], axis=0
    )
    turned = pltpu.roll(whole, lax.rem(LANES - begin, LANES), 1).T
    lon_far[...] = turned[0:8, :]

    pl.semaphore_wait(barrier, len(peers))
    raw_copy().start()
    speed_copy().start()
    lon_copy(True).start()
    lon_copy(False).start()

    @pl.when(up_ok)
    def _():
        lat_copy(True).start()
        lat_far_copy(True).start()

    @pl.when(down_ok)
    def _():
        lat_copy(False).start()
        lat_far_copy(False).start()

    lon_far_copy(True).start()
    lon_far_copy(False).start()

    @pl.when(jnp.logical_not(down_ok))
    def _():
        got_up[...] = jnp.zeros_like(got_up)

    @pl.when(jnp.logical_not(up_ok))
    def _():
        got_down[...] = jnp.zeros_like(got_down)

    for ref in (mh, ml, th, tl):
        for at in (0, (chunks + 1) * pitch):
            ref[pl.ds(at, pitch), :] = jnp.zeros((pitch, ref.shape[1]), BF16)
    for copy in small:
        copy.wait()
    rates[...] = jnp.zeros_like(rates)
    rates[0:1, 0:nf] = speed[...].reshape(1, nf)
    gains[...] = jnp.broadcast_to(
        pltpu.roll(rates[...], EDGE * fi, 1).T[0 : gains.shape[0], 0:1], gains.shape
    )
    bin0 = fi * ((nf - EDGE) * nd)
    lines[...] = jnp.zeros_like(lines)
    target = (quad[...] - bin0).astype(F32)
    shift = jnp.zeros_like(target)
    for i in range(1, chunks):
        shift = shift + jnp.where(target >= float(pair * i), float(pad), 0.0)
    lines[0:2, 0:nbins] = target + shift
    lines[2:3, 0:nbins] = time_step * coef[...].reshape(1, nbins)
    weight = profile[...].reshape(1, nbins)
    lines[3:4, 0:nbins] = weight
    lines[4:6, 0:nbins] = momentum[...] * weight
    lines[...] = pltpu.roll(lines[...], lax.rem(span - bin0, span), 1)
    cols[...] = jnp.full_like(cols, -1.0)
    for k in range(-(-chunks * pair // LANES)):
        block = lines[:, LANES * k : LANES * k + LANES].T
        at = LANES * k
        while at < min(LANES * (k + 1), chunks * pair):
            c = at // pair
            stop = min(pair * (c + 1), LANES * (k + 1))
            cols[at + pad * c : stop + pad * c, :] = block[at - LANES * k : stop - LANES * k]
            at = stop
    for k in range(span // LANES):
        lines[:, LANES * k : LANES * k + LANES] = cols[LANES * k : LANES * k + LANES, :].T
    turned = waves[...].T
    table[pl.ds(0, pair), :] = jnp.broadcast_to(turned[0:pair, 0:1], (pair, LANES))
    table[pl.ds(pair, pair), :] = jnp.broadcast_to(turned[0:pair, 1:2], (pair, LANES))

    lanes = lax.broadcasted_iota(jnp.int32, (pitch, reach), 1)
    below = lax.broadcasted_iota(jnp.int32, (pitch, reach), 0)
    own_bin = lanes == below + pitch

    def build(c, carry):
        at = pl.multiple_of(pitch * c, 8)
        where = (lanes + (at - pitch)).astype(F32)
        for i in range(2):
            chosen = jnp.where(cols[pl.ds(at, pitch), i : i + 1] == where, 1.0, 0.0)
            pick[pl.ds(pl.multiple_of(2 * at + pitch * i, 16), pitch), :] = chosen.astype(BF16)
        row = (below + at).astype(F32)
        line = pltpu.roll(lines[...], lax.rem(span + pitch - at, span), 1)
        given = jnp.where(own_bin, -2.0, 0.0)
        for i in range(2):
            given = given + jnp.where(line[i : i + 1, :reach] == row, 1.0, 0.0)
        put[pl.ds(pl.multiple_of(at, 16), pitch), :] = given.astype(BF16)
        for i, ref in enumerate((coefs, shapes, weight0, weight1)):
            ref[pl.ds(at, pitch), :] = jnp.broadcast_to(
                cols[pl.ds(at, pitch), 2 + i : 3 + i], (pitch, LANES)
            )
        mf[pl.ds(at + pair, pad), :] = jnp.zeros((pad, mf.shape[1]), F32)
        return carry

    lax.fori_loop(0, chunks, build, 0)
    sea = mask[...].astype(F32)

    def propagate(c, outer, gain, halo, sums):
        base = pl.multiple_of(c * (pair * rows), 8)
        at = pl.multiple_of(c * pitch, 16)
        store = pl.multiple_of(c * pitch + pitch, 16)
        sums = list(sums)
        held = {}
        for j in range(groups):
            low, high = 8 * j < nd, 8 * j + 8 > nd
            if low and high:
                g = jnp.where(eight < nd - 8 * j, gain[0], gain[1])
            else:
                g = jnp.broadcast_to(gain[0] if low else gain[1], (8, LANES))
            ax = g * table[8 * j : 8 * j + 8, :]
            ay = g * table[pair + 8 * j : pair + 8 * j + 8, :]
            stay = 1.0 - ax - ay
            e = [x[pl.ds(base + 8 * rows * j + r, 8, stride=rows), :] for r in range(rows)]
            if sums:
                w0, w1 = weight0[pl.ds(at + 8 * j, 8), :], weight1[pl.ds(at + 8 * j, 8), :]
            for r in range(rows):
                rim = lane == choose(forward[j], lambda: 0, lambda: LANES - 1)
                nx = choose(
                    forward[j],
                    lambda: pltpu.roll(e[r], 1, 1),
                    lambda: pltpu.roll(e[r], LANES - 1, 1),
                )
                nx = jnp.where(rim, halo(r, j), nx)
                ny = choose(
                    southern[j],
                    lambda: e[r - 1] if r > 0 else outer(j),
                    lambda: e[r + 1] if r < rows - 1 else outer(j),
                )
                m = (stay * e[r] + ax * nx + ay * ny) * sea[r : r + 1, :]
                mf[pl.ds(at + 8 * j, 8), r * LANES : (r + 1) * LANES] = m
                held[j, r] = m
                if sums:
                    for i, v in enumerate((m, m * w0, m * w1)):
                        sums[3 * r + i] = sums[3 * r + i] + v
                if j % 2 == 1 or j == groups - 1:
                    start = j if j % 2 == 0 else j - 1
                    both = [held[start, r], held[j, r] if j > start else jnp.zeros_like(m)]
                    hi, lw = split(jnp.concatenate(both, axis=0))
                    mh[pl.ds(store + 8 * start, 16), r * LANES : (r + 1) * LANES] = hi
                    ml[pl.ds(store + 8 * start, 16), r * LANES : (r + 1) * LANES] = lw
        return tuple(sums)

    def interact(c, carry):
        at = pl.multiple_of(c * pitch, 16)
        lhs = pick[pl.ds(pl.multiple_of(2 * at, 16), 2 * pitch), :window]
        both = jnp.dot(lhs, mh[pl.ds(at, window), :], preferred_element_type=F32)
        both = both + jnp.dot(lhs, ml[pl.ds(at, window), :], preferred_element_type=F32)
        third, fourth = both[:pitch], both[pitch:]
        e = mf[pl.ds(at, pitch), :]
        scale = jnp.concatenate([coefs[pl.ds(at, pitch), :]] * rows, axis=1)
        product = third * fourth
        moved = (scale * e) * (e * (third + fourth) - (product + product))
        hi, lw = split(moved)
        to = pl.multiple_of(at + pitch, 16)
        th[pl.ds(to, pitch), :] = hi
        tl[pl.ds(to, pitch), :] = lw
        return carry

    def finish(c, carry):
        at = pl.multiple_of(c * pitch, 16)
        lhs = put[pl.ds(at, pitch), :window]
        back = jnp.dot(lhs, th[pl.ds(at, window), :], preferred_element_type=F32)
        back = back + jnp.dot(lhs, tl[pl.ds(at, window), :], preferred_element_type=F32)
        shape = shapes[pl.ds(at, pair), :]
        to = (c - first) * (pair * rows)
        for r in range(rows):
            here = slice(r * LANES, (r + 1) * LANES)
            e = mf[pl.ds(at, pair), here]
            growth = 1.0 + shape * (time_step * wind[r : r + 1, :])
            result[pl.ds(to + r, pair, stride=rows), :] = e * growth + back[:pair, here]
        return carry

    def receive(ref, first_row, where):
        for i in range(len(where)):
            at = first_row + half * where[i]
            ref[pl.ds(nd * i, half), :] = got_up[pl.ds(at, half), :]
            ref[pl.ds(nd * i + half, half), :] = got_down[pl.ds(at, half), :]

    @pl.when(down_ok)
    def _():
        lat_copy(True).wait_recv()

    @pl.when(up_ok)
    def _():
        lat_copy(False).wait_recv()

    receive(edge, far_lat, [places[f] for f in range(nf)])
    lon_copy(True).wait_recv()
    lon_copy(False).wait_recv()
    for j in range(groups):
        here = slice(8 * j, 8 * j + 8)
        got_left[here, :] = choose(
            forward[j],
            lambda: got_left[here, :],
            lambda: pltpu.roll(got_right[here, :], LANES - 1, 1),
        )

    def own(c, sums):
        def halo(r, j):
            return pltpu.roll(got_left[8 * j : 8 * j + 8, :], LANES - (c * rows + r), 1)

        def outer(j):
            return edge[pl.ds(pl.multiple_of((c - first) * pair, 8) + 8 * j, 8), :]

        gain = [gains[pl.ds(2 * c + i, 1), :] for i in range(2)]
        return propagate(c, outer, gain, halo, sums)

    sums = tuple(jnp.zeros((8, LANES), F32) for _ in range(3 * rows))
    sums = lax.fori_loop(first, first + own_chunks, own, sums)

    all_rows = n_lat * rows
    part[pl.ds(0, 8), :] = jnp.zeros((8, LANES), F32)
    ids = (lo * LANES + lax.broadcasted_iota(jnp.int32, (all_rows, LANES), 1)) * all_rows
    ids = ids + lax.broadcasted_iota(jnp.int32, (all_rows, LANES), 0)
    totals = [jnp.zeros((all_rows, LANES), F32) for _ in range(2)]
    for r in range(rows):
        part[r : r + 1, :] = jnp.sum(sums[3 * r], axis=0, keepdims=True)
        hit = cells[r : r + 1, :] == ids
        for i in range(2):
            tau = wind[r : r + 1, :] * jnp.sum(sums[3 * r + 1 + i], axis=0, keepdims=True)
            totals[i] = totals[i] + jnp.where(hit, tau, 0.0)
    for i in range(2):
        part[pl.ds(8 + i * all_rows, all_rows), :] = totals[i]
    for s in range(len(group)):
        part_copy(s).start()

    lax.fori_loop(
        2 * first - fi, chunks - far_chunks - 1 + fi * (far_chunks + 1), interact, 0
    )
    lax.fori_loop(2 * first, chunks - 2 * far_chunks + fi * 2 * far_chunks, finish, 0)

    for s in range(len(group)):
        part_copy(s).wait()
    en = part[pl.ds(0, 8), :]
    st = part[pl.ds(8, 2 * all_rows), :]
    for s, (dl, _) in enumerate(group):
        if dl == 0:
            en = en + parts[s, pl.ds(0, 8), :]
        st = st + parts[s, pl.ds(8, 2 * all_rows), :]
    loss = time_step * dissip[...] * (en[0:rows] / nbins)
    share = (LANES // n_freq) * all_rows
    cell = lax.broadcasted_iota(jnp.int32, (LANES, share), 1)
    first_cell = (lax.broadcasted_iota(jnp.int32, (LANES, share), 0) - fi * (LANES // n_freq)) * all_rows
    inside = jnp.logical_and(cell >= first_cell, cell < first_cell + all_rows)
    wide = jnp.dot(
        st, jnp.where(inside, 1.0, 0.0),
        precision=lax.Precision.HIGHEST, preferred_element_type=F32,
    )
    place = lax.broadcasted_iota(jnp.int32, (all_rows, share), 1) & (all_rows - 1)
    own_row = place == lax.broadcasted_iota(jnp.int32, (all_rows, share), 0)
    for i in range(2):
        picked = jnp.where(own_row, wide[i * all_rows : (i + 1) * all_rows], 0.0)
        stress[i : i + 1, :] = jnp.sum(picked, axis=0, keepdims=True)

    speed_copy().wait_recv()
    rates[0:1, 0:nf] = speed_far[...].reshape(1, nf)
    gains_far[...] = jnp.broadcast_to(
        pltpu.roll(rates[...], fi * (LANES - (nf - EDGE)), 1).T[0:8, 0:1], gains_far.shape
    )

    @pl.when(down_ok)
    def _():
        lat_far_copy(True).wait_recv()

    @pl.when(up_ok)
    def _():
        lat_far_copy(False).wait_recv()

    receive(edge_far, 0, list(range(EDGE)))
    lon_far_copy(True).wait_recv()
    lon_far_copy(False).wait_recv()
    left, right = far_left[...].T, far_right[...].T
    for j in range(groups):
        here = slice(8 * j, 8 * j + 8)
        ahead = eight[:, 0:8] < 0
        for i, flag in enumerate(forward[j]):
            if flag:
                ahead = jnp.logical_or(ahead, eight[:, 0:8] == i)
        cols_far[here, :] = jnp.where(ahead, left[here], right[here])
    raw_copy().wait_recv()

    for u in range(far_chunks):
        def halo(r, j):
            k = u * rows + r
            return jnp.broadcast_to(cols_far[8 * j : 8 * j + 8, k : k + 1], (8, LANES))

        def outer(j):
            return edge_far[pair * u + 8 * j : pair * u + 8 * j + 8, :]

        gain = [gains_far[2 * u + i : 2 * u + i + 1, :] for i in range(2)]
        propagate(far_first + u, outer, gain, halo, ())

    late = (chunks - far_chunks - 1) * other + fi
    lax.fori_loop(late, late + 2, interact, 0)
    late = (chunks - 2 * far_chunks) * other + fi * far_chunks
    lax.fori_loop(late, late + 2, finish, 0)

    def settle(t, carry):
        at = pl.multiple_of((t + first) * pitch, 8)
        for r in range(rows):
            spot = pl.ds(t * (pair * rows) + r, pair, stride=rows)
            e = mf[pl.ds(at, pair), r * LANES : (r + 1) * LANES]
            result[spot, :] = result[spot, :] - e * loss[r : r + 1, :]
        return carry

    lax.fori_loop(0, own_chunks, settle, 0)

    raw_copy().wait_send()
    speed_copy().wait_send()
    for flag in (True, False):
        lon_copy(flag).wait_send()
        lon_far_copy(flag).wait_send()

    @pl.when(up_ok)
    def _():
        lat_copy(True).wait_send()
        lat_far_copy(True).wait_send()

    @pl.when(down_ok)
    def _():
        lat_copy(False).wait_send()
        lat_far_copy(False).wait_send()


def write_kernel(result, stress, result_out, stress_out, sems):
    pieces = sems.shape[0] - 1
    size = result.shape[0] // pieces
    copies = [pltpu.make_async_copy(stress, stress_out, sems.at[pieces])]
    for i in range(pieces):
        here = pl.ds(size * i, size)
        copies.append(pltpu.make_async_copy(result.at[here], result_out.at[here], sems.at[i]))
    for copy in copies:
        copy.start()
    for copy in copies:
        copy.wait()


def local(
    axes,
    spectrum,
    group_speed,
    sea_mask,
    wind_growth,
    dissipation,
    wind_profile,
    nonlinear_coef,
    momentum,
    quadruplet,
    ocean_cell,
):
    n_lat, n_lon, n_freq = axes
    nf, nd, rows, width = spectrum.shape
    nbins = wind_profile.shape[0]
    assert n_freq == 2 and nf % 2 == 0 and width == LANES
    band, pair, half = nf * nd, 2 * nd, nd // 2
    pitch = round_up(pair, 16)
    chunks = nf // 2 + EDGE // 2
    all_rows = n_lat * rows
    angles = (np.float32(2.0 * np.pi) * np.arange(nd, dtype=np.float32) / np.float32(nd)).astype(
        np.float32
    )
    cosines, sines = np.cos(angles), np.sin(angles)
    waves = np.zeros((8, LANES), np.float32)
    waves[0, :pair], waves[1, :pair] = np.tile(np.abs(cosines), 2), np.tile(np.abs(sines), 2)

    packed = round_up(nf * half, 8)
    far_lat = EDGE * half
    peers = n_lat * n_freq - 1
    small = 8 + 2 * all_rows
    share = (width // n_freq) * all_rows
    span = round_up(max(nbins, (chunks + 2) * pitch), LANES)
    reach = round_up(3 * pitch, LANES)
    vmem = pl.BlockSpec(memory_space=VMEM)
    hbm = pl.BlockSpec(memory_space=pltpu.HBM)
    sizes = (n_lat, n_lon, n_freq, nf, nd, rows, nbins)
    dma = pltpu.SemaphoreType.DMA
    smalls = (
        group_speed,
        jnp.asarray(waves),
        wind_profile,
        nonlinear_coef,
        momentum,
        quadruplet,
        sea_mask,
        wind_growth,
        dissipation,
        ocean_cell,
    )
    out, ocean = pl.pallas_call(
        functools.partial(wave_kernel, sizes, (cosines, sines)),
        out_shape=(
            jax.ShapeDtypeStruct((band * rows, width), F32),
            jax.ShapeDtypeStruct((2, share), F32),
        ),
        in_specs=[hbm] * 11,
        out_specs=(vmem, vmem),
        scratch_shapes=[VMEM(a.shape, a.dtype) for a in smalls]
        + [
            VMEM((chunks * pair * rows, width), F32),
            VMEM((chunks * pitch, rows * width), F32),
            VMEM(((chunks + 2) * pitch, rows * width), BF16),
            VMEM(((chunks + 2) * pitch, rows * width), BF16),
            VMEM(((chunks + 2) * pitch, rows * width), BF16),
            VMEM(((chunks + 2) * pitch, rows * width), BF16),
            VMEM((2 * chunks * pitch, reach), BF16),
            VMEM((chunks * pitch, reach), BF16),
            VMEM((2 * pair, width), F32),
            VMEM((8, width), F32),
            VMEM((span, 8), F32),
            VMEM((8, span), F32),
            VMEM((chunks * pitch, width), F32),
            VMEM((chunks * pitch, width), F32),
            VMEM((chunks * pitch, width), F32),
            VMEM((chunks * pitch, width), F32),
            VMEM((round_up(nf + EDGE, 8), width), F32),
            VMEM((8, width), F32),
            VMEM(group_speed.shape, F32),
            VMEM((packed, width), F32),
            VMEM((packed, width), F32),
            VMEM((far_lat + packed, width), F32),
            VMEM((far_lat + packed, width), F32),
            VMEM((band, width), F32),
            VMEM((EDGE * nd, width), F32),
            VMEM((pair, width), F32),
            VMEM((pair, width), F32),
            VMEM((pair, width), F32),
            VMEM((8, width), F32),
            VMEM((8, width), F32),
            VMEM((8, width), F32),
            VMEM((pair, 8), F32),
            VMEM((small, width), F32),
            VMEM((peers, small, width), F32),
            dma, dma((len(smalls),)),
            dma((2,)), dma((2,)), dma((4,)), dma((4,)), dma((4,)), dma((4,)),
            dma((peers,)), dma((peers,)),
        ],
        compiler_params=pltpu.CompilerParams(
            collective_id=0, has_side_effects=True, vmem_limit_bytes=32 << 20
        ),
    )(
        *[
            pltpu.with_memory_space_constraint(a, pltpu.HBM)
            for a in (spectrum.reshape(band * rows, width), *smalls)
        ]
    )
    out, ocean = pl.pallas_call(
        write_kernel,
        out_shape=(
            jax.ShapeDtypeStruct((band * rows, width), F32),
            jax.ShapeDtypeStruct((2, share), F32),
        ),
        in_specs=[vmem, vmem],
        out_specs=(hbm, hbm),
        scratch_shapes=[dma((5,))],
        compiler_params=pltpu.CompilerParams(vmem_limit_bytes=1 << 20),
    )(out, ocean)
    return out.reshape(spectrum.shape), ocean.T


def solution(mesh):
    axes = tuple(mesh.shape[a] for a in ("lat", "lon", "freq"))
    return jax.shard_map(
        functools.partial(local, axes),
        mesh=mesh,
        in_specs=(
            P("freq", None, "lat", "lon"),
            P("freq"),
            P("lat", "lon"),
            P("lat", "lon"),
            P("lat", "lon"),
            P(),
            P(),
            P(),
            P(),
            P("lat", "lon"),
        ),
        out_specs=(P("freq", None, "lat", "lon"), P(("lon", "freq"), None)),
        check_vma=False,
    )
```

time: 24.8 us -> 20.3 us (0.82)
  Pallas kernels: 22.3 us -> 19.5 us
  local copies, waits for them, and re-layouts: 1.66 us -> 0 us
    pallas_call x1 -> x2, Pallas kernels: 22.3 us -> 19.5 us  [the longest x1 18.4 us: local(): pl.pallas_call(functools.partial(wave_kernel, sizes, (cosines, sines)), o...]
    unnamed x2 -> x0, local copies, waits for them, and re-layouts: 1.66 us -> none
where the time goes in v1:
time: 20.3 us; the launch traced here: 20.1 us
  Pallas kernels  19.5 us (96%)
  between operations  0.64 us (3%)
    pallas_call x1, Pallas kernels, local(): pl.pallas_call(functools.partial(wave_kernel, sizes, (cosines, sines)), o...  18.4 us
    pallas_call x1, Pallas kernels, local(): pl.pallas_call(write_kernel, out_shape=(jax.ShapeDtypeStruct((band * rows...  1.1 us

profile of v1, /device:TPU:0, one launch (start us, length us, event | category | flops | bytes accessed | tf_op | source)
XLA Modules:
  0.0 20.1 jit_solution(16120320823820033213)
XLA Ops:
  0.6 18.4 %shard_map.122 = (f32[2592,128]{1,0:T(8,128)S(1)}, f32[2,512]{1,0:T(2,128)S(1)}) custom-call(f32[2592,128]{1,0:T(8,128)} %bitcast.3, f32[18]{0:T(128)} %refs_0_.1, f32[8,128]{1,0:T(8,128)} %constant.2.clone.refs_1_, f32[1296]{0:T(1024)} %refs_2_.1, f32[1296]{0:T(1024)} %refs_3_.1, f32[2,1296]{1,0:T(2,128)} %refs_4_.1, s32[2,1296]{1,0:T(2,128)} %refs_5_.1, ...), custom_call_target="tpu_custom_call" | custom-call | tf_op jit(solution)/shard_map/pallas_call | solution.py:591
  19.0 1.1 %shard_map.123 = (f32[2592,128]{1,0:T(8,128)}, f32[2,512]{1,0:T(2,128)}) custom-call(f32[2592,128]{1,0:T(8,128)S(1)} %get-tuple-element.6.result, f32[2,512]{1,0:T(2,128)S(1)} %get-tuple-element.7.stress), custom_call_target="tpu_custom_call" | custom-call | tf_op jit(solution)/shard_map/pallas_call | solution.py:648

commit v2 on v1

--- a/solution.py
+++ b/solution.py
@@ -28,6 +28,12 @@
 def split(v):
     high = v.astype(BF16)
     return high, (v - high.astype(F32)).astype(BF16)
+
+
+def thirds(v):
+    high, low = split(v)
+    rest = v - high.astype(F32) - low.astype(F32)
+    return high, low, rest.astype(BF16)
 
 
 def wave_kernel(sizes, angles, spectrum, *refs):
@@ -38,14 +44,15 @@
     (
         x, mf, mh, ml, th, tl, pick, put, table, rates, cols, lines, coefs, shapes, weight0, weight1,
         gains, gains_far, speed_far, pack_up, pack_down, got_up, got_down, edge, edge_far,
-        lon_pack, got_left, got_right, lon_far, far_left, far_right, cols_far, part, parts,
-        load_sem, small_sem, raw_send, raw_recv, lat_send, lat_recv, lon_send, lon_recv,
-        part_send, part_recv,
+        lon_pack, got_left, got_right, lon_far, far_left, far_right, cols_far, spread_out, energy, energy_got, tau_own, taus,
+        load_sem, small_sem, ready_sem, raw_send, raw_recv, lat_send, lat_recv, lon_send, lon_recv,
+        sum_send, sum_recv, tau_send, tau_recv,
     ) = refs
     n_lat, n_lon, n_freq, nf, nd, rows, nbins = sizes
     half = nd // 2
     pair = 2 * nd
     band = nf * nd
+    all_rows = n_lat * rows
     pitch = round_up(pair, 16)
     pad = pitch - pair
     own_chunks = nf // 2
@@ -63,40 +70,53 @@
     far_first = own_chunks * other
 
     own_rows = pl.multiple_of(first * (pair * rows), 8)
-    load = pltpu.make_async_copy(spectrum, x.at[pl.ds(own_rows, band * rows)], load_sem)
-    load.start()
     small = [
         pltpu.make_async_copy(a, b, small_sem.at[i])
         for i, (a, b) in enumerate(zip(sources, inputs))
     ]
-    for copy in small:
+    step = 3 if own_chunks % 3 == 0 else 1
+    loads = []
+    for i in range(own_chunks // step):
+        count = step * pair * rows
+        loads.append(
+            pltpu.make_async_copy(
+                spectrum.at[pl.ds(i * count, count)], x.at[pl.ds(own_rows + i * count, count)],
+                load_sem.at[i],
+            )
+        )
+    for copy in loads + small:
         copy.start()
 
     east, west = lax.rem(lo + 1, n_lon), lax.rem(lo + n_lon - 1, n_lon)
     group = []
     for s in range(1, n_lat * n_freq):
         dl, df = divmod(s, n_freq)
-        group.append(
-            (dl, {"lat": lax.rem(li + dl, n_lat), "freq": lax.rem(fi + df, n_freq)})
-        )
+        group.append({"lat": lax.rem(li + dl, n_lat), "freq": lax.rem(fi + df, n_freq)})
     barrier = pltpu.get_barrier_semaphore()
-    peers = [{"lon": east}, {"lon": west}]
-    peers += [{"lon": east, "freq": other}, {"lon": west, "freq": other}]
-    peers += [g for _, g in group]
-    for peer in peers:
+    beside = [{"lon": east}, {"lon": west}]
+    beside += [{"lon": east, "freq": other}, {"lon": west, "freq": other}]
+    odd = lax.rem(lo, 2)
+    for peer in group:
         pl.semaphore_signal(barrier, inc=1, device_id=peer, device_id_type=MESH)
+
+    @pl.when(odd == 0)
+    def _():
+        for peer in beside:
+            pl.semaphore_signal(barrier, inc=1, device_id=peer, device_id_type=MESH)
 
     packed = pack_up.shape[0]
     far_lat = EDGE * half
     up_ok, down_ok = li < n_lat - 1, li > 0
 
-    def raw_copy():
-        count = EDGE * nd * rows
-        src = pl.multiple_of(other * ((nf - EDGE) * nd * rows), 8)
-        dst = pl.multiple_of(fi * (band * rows), 8)
+    def raw_copy(near):
+        count = EDGE // 2 * nd * rows
+        half_at = (other if near else fi) * count
+        src = pl.multiple_of(other * ((nf - EDGE) * nd * rows) + half_at, 8)
+        dst = pl.multiple_of(fi * (band * rows) + half_at, 8)
+        i = 2 if near else 0
         return pltpu.make_async_remote_copy(
             spectrum.at[pl.ds(src, count)], x.at[pl.ds(dst, count)],
-            raw_send.at[0], raw_recv.at[0], device_id={"freq": other}, device_id_type=MESH,
+            raw_send.at[i], raw_recv.at[i], device_id={"freq": other}, device_id_type=MESH,
         )
 
     def speed_copy():
@@ -136,10 +156,16 @@
             device_id={"lon": east if to_east else west, "freq": other}, device_id_type=MESH,
         )
 
-    def part_copy(s):
+    def energy_copy():
         return pltpu.make_async_remote_copy(
-            part, parts.at[s], part_send.at[s], part_recv.at[s],
-            device_id=group[s][1], device_id_type=MESH,
+            energy, energy_got, sum_send.at[0], sum_recv.at[0],
+            device_id={"freq": other}, device_id_type=MESH,
+        )
+
+    def tau_copy(s):
+        return pltpu.make_async_remote_copy(
+            tau_own, taus.at[s], tau_send.at[s], tau_recv.at[s],
+            device_id=group[s], device_id_type=MESH,
         )
 
     def signs(values, j):
@@ -168,19 +194,20 @@
 
     pack_up[pl.ds(packed - 8, 8), :] = jnp.zeros((8, LANES), F32)
     pack_down[pl.ds(packed - 8, 8), :] = jnp.zeros((8, LANES), F32)
-    load.wait()
-    for f in range(nf):
-        at = half * places[f]
-        base = own_rows + nd * f * rows
-        pack_up[pl.ds(at, half), :] = x[pl.ds(base + rows - 1, half, stride=rows), :]
-        pack_down[pl.ds(at, half), :] = x[pl.ds(base + half * rows, half, stride=rows), :]
-
-    step = 3 if own_chunks % 3 == 0 else 1
-
-    def pack_step(t, acc):
-        acc = list(acc)
+    sums = [jnp.zeros((8, LANES), F32) for _ in range(groups)]
+    for i, copy in enumerate(loads):
+        if i == len(loads) - 1:
+            pl.semaphore_wait(barrier, len(group) + odd * len(beside))
+            speed_copy().start()
+            raw_copy(True).start()
+        copy.wait()
+        for f in range(2 * step * i, 2 * step * (i + 1)):
+            at = half * places[f]
+            base = own_rows + nd * f * rows
+            pack_up[pl.ds(at, half), :] = x[pl.ds(base + rows - 1, half, stride=rows), :]
+            pack_down[pl.ds(at, half), :] = x[pl.ds(base + half * rows, half, stride=rows), :]
         for u in range(step):
-            c = t * step + u + first
+            c = i * step + u + first
             base = pl.multiple_of(c * (pair * rows), 8)
             for r in range(rows):
                 k = c * rows + r
@@ -191,15 +218,12 @@
                         lambda: jnp.where(lane == LANES - 1, e, 0.0),
                         lambda: jnp.where(lane == 0, e, 0.0),
                     )
-                    acc[j] = acc[j] + pltpu.roll(z, k, 1)
-        return tuple(acc)
-
-    sums = lax.fori_loop(
-        0, own_chunks // step, pack_step, tuple(jnp.zeros((8, LANES), F32) for _ in range(groups))
-    )
+                    sums[j] = sums[j] + pltpu.roll(z, k, 1)
+
     for j in range(groups):
         aligned = choose(forward[j], lambda: pltpu.roll(sums[j], 1, 1), lambda: sums[j])
         lon_pack[8 * j : 8 * j + 8, :] = aligned
+
     begin = (first + (own_chunks - far_chunks) * other) * rows
     whole = jnp.concatenate(
         [lon_pack[...], jnp.zeros((LANES - pair, LANES), F32)], axis=0
@@ -207,36 +231,32 @@
     turned = pltpu.roll(whole, lax.rem(LANES - begin, LANES), 1).T
     lon_far[...] = turned[0:8, :]
 
-    pl.semaphore_wait(barrier, len(peers))
-    raw_copy().start()
-    speed_copy().start()
-    lon_copy(True).start()
-    lon_copy(False).start()
-
     @pl.when(up_ok)
     def _():
         lat_copy(True).start()
+
+    @pl.when(down_ok)
+    def _():
+        lat_copy(False).start()
+
+    @pl.when(up_ok)
+    def _():
         lat_far_copy(True).start()
 
     @pl.when(down_ok)
     def _():
-        lat_copy(False).start()
         lat_far_copy(False).start()
 
-    lon_far_copy(True).start()
-    lon_far_copy(False).start()
-
-    @pl.when(jnp.logical_not(down_ok))
-    def _():
-        got_up[...] = jnp.zeros_like(got_up)
-
-    @pl.when(jnp.logical_not(up_ok))
-    def _():
-        got_down[...] = jnp.zeros_like(got_down)
-
-    for ref in (mh, ml, th, tl):
-        for at in (0, (chunks + 1) * pitch):
-            ref[pl.ds(at, pitch), :] = jnp.zeros((pitch, ref.shape[1]), BF16)
+    raw_copy(False).start()
+
+    @pl.when(odd == 1)
+    def _():
+        for peer in beside:
+            pl.semaphore_signal(ready_sem, inc=1, device_id=peer, device_id_type=MESH)
+        for to_east in (True, False):
+            lon_copy(to_east).start()
+            lon_far_copy(to_east).start()
+
     for copy in small:
         copy.wait()
     rates[...] = jnp.zeros_like(rates)
@@ -271,6 +291,27 @@
     table[pl.ds(0, pair), :] = jnp.broadcast_to(turned[0:pair, 0:1], (pair, LANES))
     table[pl.ds(pair, pair), :] = jnp.broadcast_to(turned[0:pair, 1:2], (pair, LANES))
 
+    def send_columns():
+        pl.semaphore_wait(ready_sem, len(beside))
+        for to_east in (True, False):
+            lon_copy(to_east).start()
+            lon_far_copy(to_east).start()
+
+    @pl.when(jnp.logical_and(odd == 0, lo > 0))
+    def _():
+        send_columns()
+
+    @pl.when(jnp.logical_not(down_ok))
+    def _():
+        got_up[...] = jnp.zeros_like(got_up)
+
+    @pl.when(jnp.logical_not(up_ok))
+    def _():
+        got_down[...] = jnp.zeros_like(got_down)
+
+    for ref in (mh, ml, th, tl):
+        for at in (0, (chunks + 1) * pitch):
+            ref[pl.ds(at, pitch), :] = jnp.zeros((pitch, ref.shape[1]), BF16)
     lanes = lax.broadcasted_iota(jnp.int32, (pitch, reach), 1)
     below = lax.broadcasted_iota(jnp.int32, (pitch, reach), 0)
     own_bin = lanes == below + pitch
@@ -295,13 +336,39 @@
         return carry
 
     lax.fori_loop(0, chunks, build, 0)
+    share = (LANES // n_freq) * all_rows
+    cell = lax.broadcasted_iota(jnp.int32, (LANES, share), 1)
+    first_cell = (lax.broadcasted_iota(jnp.int32, (LANES, share), 0) - fi * (LANES // n_freq)) * all_rows
+    inside = jnp.logical_and(cell >= first_cell, cell < first_cell + all_rows)
+    spread_out[...] = jnp.where(inside, 1.0, 0.0).astype(BF16)
+
+    @pl.when(lo == 0)
+    def _():
+        send_columns()
+
     sea = mask[...].astype(F32)
 
-    def propagate(c, outer, gain, halo, sums):
+    inner, rim_rows = list(range(1, rows - 1)), [0, rows - 1]
+    slot = {r: i for i, r in enumerate(inner + rim_rows)}
+    whole_cols = slice(0, rows * LANES)
+    inner_cols, rim_cols = slice(0, len(inner) * LANES), slice(len(inner) * LANES, rows * LANES)
+
+    def columns(r):
+        return slice(slot[r] * LANES, slot[r] * LANES + LANES)
+
+    def upwind(e, j):
+        if all(forward[j]):
+            return pltpu.roll(e, 1, 1)
+        if not any(forward[j]):
+            return pltpu.roll(e, LANES - 1, 1)
+        at = lane + jnp.where(rows_of(forward[j]), LANES - 1, 1)
+        return jnp.take_along_axis(e, at & (LANES - 1), axis=1)
+
+    def propagate(c, outer, gain, halo, row_set, sums):
         base = pl.multiple_of(c * (pair * rows), 8)
         at = pl.multiple_of(c * pitch, 16)
         store = pl.multiple_of(c * pitch + pitch, 16)
-        sums = list(sums)
+        sums = dict(sums)
         held = {}
         for j in range(groups):
             low, high = 8 * j < nd, 8 * j + 8 > nd
@@ -315,62 +382,70 @@
             e = [x[pl.ds(base + 8 * rows * j + r, 8, stride=rows), :] for r in range(rows)]
             if sums:
                 w0, w1 = weight0[pl.ds(at + 8 * j, 8), :], weight1[pl.ds(at + 8 * j, 8), :]
-            for r in range(rows):
+            for r in row_set:
                 rim = lane == choose(forward[j], lambda: 0, lambda: LANES - 1)
-                nx = choose(
-                    forward[j],
-                    lambda: pltpu.roll(e[r], 1, 1),
-                    lambda: pltpu.roll(e[r], LANES - 1, 1),
-                )
-                nx = jnp.where(rim, halo(r, j), nx)
+                nx = jnp.where(rim, halo(r, j), upwind(e[r], j))
                 ny = choose(
                     southern[j],
                     lambda: e[r - 1] if r > 0 else outer(j),
                     lambda: e[r + 1] if r < rows - 1 else outer(j),
                 )
                 m = (stay * e[r] + ax * nx + ay * ny) * sea[r : r + 1, :]
-                mf[pl.ds(at + 8 * j, 8), r * LANES : (r + 1) * LANES] = m
+                mf[pl.ds(at + 8 * j, 8), columns(r)] = m
                 held[j, r] = m
                 if sums:
                     for i, v in enumerate((m, m * w0, m * w1)):
-                        sums[3 * r + i] = sums[3 * r + i] + v
+                        sums[r, i] = sums[r, i] + v
                 if j % 2 == 1 or j == groups - 1:
                     start = j if j % 2 == 0 else j - 1
                     both = [held[start, r], held[j, r] if j > start else jnp.zeros_like(m)]
                     hi, lw = split(jnp.concatenate(both, axis=0))
-                    mh[pl.ds(store + 8 * start, 16), r * LANES : (r + 1) * LANES] = hi
-                    ml[pl.ds(store + 8 * start, 16), r * LANES : (r + 1) * LANES] = lw
-        return tuple(sums)
-
-    def interact(c, carry):
+                    mh[pl.ds(store + 8 * start, 16), columns(r)] = hi
+                    ml[pl.ds(store + 8 * start, 16), columns(r)] = lw
+        return sums
+
+    def interact(c, cs):
+        width = (cs.stop - cs.start) // LANES
         at = pl.multiple_of(c * pitch, 16)
         lhs = pick[pl.ds(pl.multiple_of(2 * at, 16), 2 * pitch), :window]
-        both = jnp.dot(lhs, mh[pl.ds(at, window), :], preferred_element_type=F32)
-        both = both + jnp.dot(lhs, ml[pl.ds(at, window), :], preferred_element_type=F32)
+        both = jnp.dot(lhs, mh[pl.ds(at, window), cs], preferred_element_type=F32)
+        both = both + jnp.dot(lhs, ml[pl.ds(at, window), cs], preferred_element_type=F32)
         third, fourth = both[:pitch], both[pitch:]
-        e = mf[pl.ds(at, pitch), :]
-        scale = jnp.concatenate([coefs[pl.ds(at, pitch), :]] * rows, axis=1)
+        e = mf[pl.ds(at, pitch), cs]
+        scale = jnp.concatenate([coefs[pl.ds(at, pitch), :]] * width, axis=1)
         product = third * fourth
         moved = (scale * e) * (e * (third + fourth) - (product + product))
         hi, lw = split(moved)
         to = pl.multiple_of(at + pitch, 16)
-        th[pl.ds(to, pitch), :] = hi
-        tl[pl.ds(to, pitch), :] = lw
-        return carry
-
-    def finish(c, carry):
+        th[pl.ds(to, pitch), cs] = hi
+        tl[pl.ds(to, pitch), cs] = lw
+
+    def finish(c, cs, loss=None):
         at = pl.multiple_of(c * pitch, 16)
         lhs = put[pl.ds(at, pitch), :window]
-        back = jnp.dot(lhs, th[pl.ds(at, window), :], preferred_element_type=F32)
-        back = back + jnp.dot(lhs, tl[pl.ds(at, window), :], preferred_element_type=F32)
+        back = jnp.dot(lhs, th[pl.ds(at, window), cs], preferred_element_type=F32)
+        back = back + jnp.dot(lhs, tl[pl.ds(at, window), cs], preferred_element_type=F32)
         shape = shapes[pl.ds(at, pair), :]
         to = (c - first) * (pair * rows)
         for r in range(rows):
-            here = slice(r * LANES, (r + 1) * LANES)
+            here = columns(r)
+            if here.start < cs.start or here.stop > cs.stop:
+                continue
             e = mf[pl.ds(at, pair), here]
-            growth = 1.0 + shape * (time_step * wind[r : r + 1, :])
-            result[pl.ds(to + r, pair, stride=rows), :] = e * growth + back[:pair, here]
-        return carry
+            stay = 1.0 if loss is None else 1.0 - loss[r : r + 1, :]
+            growth = stay + shape * (time_step * wind[r : r + 1, :])
+            gain = back[:pair, here.start - cs.start : here.stop - cs.start]
+            result[pl.ds(to + r, pair, stride=rows), :] = e * growth + gain
+
+    def run(what, begin, count, cs, at_once):
+        def body(t, carry):
+            for u in range(at_once):
+                what(begin + t * at_once + u, cs)
+            return carry
+
+        lax.fori_loop(0, count // at_once, body, 0)
+        for u in range(count - count % at_once, count):
+            what(begin + u, cs)
 
     def receive(ref, first_row, where):
         for i in range(len(where)):
@@ -378,15 +453,6 @@
             ref[pl.ds(nd * i, half), :] = got_up[pl.ds(at, half), :]
             ref[pl.ds(nd * i + half, half), :] = got_down[pl.ds(at, half), :]
 
-    @pl.when(down_ok)
-    def _():
-        lat_copy(True).wait_recv()
-
-    @pl.when(up_ok)
-    def _():
-        lat_copy(False).wait_recv()
-
-    receive(edge, far_lat, [places[f] for f in range(nf)])
     lon_copy(True).wait_recv()
     lon_copy(False).wait_recv()
     for j in range(groups):
@@ -397,62 +463,61 @@
             lambda: pltpu.roll(got_right[here, :], LANES - 1, 1),
         )
 
-    def own(c, sums):
-        def halo(r, j):
-            return pltpu.roll(got_left[8 * j : 8 * j + 8, :], LANES - (c * rows + r), 1)
-
-        def outer(j):
-            return edge[pl.ds(pl.multiple_of((c - first) * pair, 8) + 8 * j, 8), :]
-
-        gain = [gains[pl.ds(2 * c + i, 1), :] for i in range(2)]
-        return propagate(c, outer, gain, halo, sums)
-
-    sums = tuple(jnp.zeros((8, LANES), F32) for _ in range(3 * rows))
-    sums = lax.fori_loop(first, first + own_chunks, own, sums)
-
-    all_rows = n_lat * rows
-    part[pl.ds(0, 8), :] = jnp.zeros((8, LANES), F32)
+    def own(row_set):
+        names = [(r, i) for r in row_set for i in range(3)]
+
+        def body(t, sums):
+            sums = dict(zip(names, sums))
+            for u in range(step):
+                c = first + t * step + u
+
+                def halo(r, j):
+                    return pltpu.roll(got_left[8 * j : 8 * j + 8, :], LANES - (c * rows + r), 1)
+
+                def outer(j):
+                    return edge[pl.ds(pl.multiple_of((c - first) * pair, 8) + 8 * j, 8), :]
+
+                gain = [gains[pl.ds(2 * c + i, 1), :] for i in range(2)]
+                sums = propagate(c, outer, gain, halo, row_set, sums)
+            return tuple(sums[n] for n in names)
+
+        zeros = tuple(jnp.zeros((8, LANES), F32) for _ in names)
+        return dict(zip(names, lax.fori_loop(0, own_chunks // step, body, zeros)))
+
+    near_first = 2 * first - fi
+    near_count = chunks - far_chunks - 1
+    last_first = 2 * first
+    last_count = chunks - 2 * far_chunks
+    sums = own(inner)
+    @pl.when(down_ok)
+    def _():
+        lat_copy(True).wait_recv()
+
+    @pl.when(up_ok)
+    def _():
+        lat_copy(False).wait_recv()
+
+    receive(edge, far_lat, [places[f] for f in range(nf)])
+    sums.update(own(rim_rows))
+
+    energy[...] = jnp.zeros((8, LANES), F32)
     ids = (lo * LANES + lax.broadcasted_iota(jnp.int32, (all_rows, LANES), 1)) * all_rows
     ids = ids + lax.broadcasted_iota(jnp.int32, (all_rows, LANES), 0)
     totals = [jnp.zeros((all_rows, LANES), F32) for _ in range(2)]
     for r in range(rows):
-        part[r : r + 1, :] = jnp.sum(sums[3 * r], axis=0, keepdims=True)
+        energy[r : r + 1, :] = jnp.sum(sums[r, 0], axis=0, keepdims=True)
         hit = cells[r : r + 1, :] == ids
         for i in range(2):
-            tau = wind[r : r + 1, :] * jnp.sum(sums[3 * r + 1 + i], axis=0, keepdims=True)
+            tau = wind[r : r + 1, :] * jnp.sum(sums[r, 1 + i], axis=0, keepdims=True)
             totals[i] = totals[i] + jnp.where(hit, tau, 0.0)
     for i in range(2):
-        part[pl.ds(8 + i * all_rows, all_rows), :] = totals[i]
+        tau_own[pl.ds(i * all_rows, all_rows), :] = totals[i]
+    energy_copy().start()
     for s in range(len(group)):
-        part_copy(s).start()
-
-    lax.fori_loop(
-        2 * first - fi, chunks - far_chunks - 1 + fi * (far_chunks + 1), interact, 0
-    )
-    lax.fori_loop(2 * first, chunks - 2 * far_chunks + fi * 2 * far_chunks, finish, 0)
-
-    for s in range(len(group)):
-        part_copy(s).wait()
-    en = part[pl.ds(0, 8), :]
-    st = part[pl.ds(8, 2 * all_rows), :]
-    for s, (dl, _) in enumerate(group):
-        if dl == 0:
-            en = en + parts[s, pl.ds(0, 8), :]
-        st = st + parts[s, pl.ds(8, 2 * all_rows), :]
-    loss = time_step * dissip[...] * (en[0:rows] / nbins)
-    share = (LANES // n_freq) * all_rows
-    cell = lax.broadcasted_iota(jnp.int32, (LANES, share), 1)
-    first_cell = (lax.broadcasted_iota(jnp.int32, (LANES, share), 0) - fi * (LANES // n_freq)) * all_rows
-    inside = jnp.logical_and(cell >= first_cell, cell < first_cell + all_rows)
-    wide = jnp.dot(
-        st, jnp.where(inside, 1.0, 0.0),
-        precision=lax.Precision.HIGHEST, preferred_element_type=F32,
-    )
-    place = lax.broadcasted_iota(jnp.int32, (all_rows, share), 1) & (all_rows - 1)
-    own_row = place == lax.broadcasted_iota(jnp.int32, (all_rows, share), 0)
-    for i in range(2):
-        picked = jnp.where(own_row, wide[i * all_rows : (i + 1) * all_rows], 0.0)
-        stress[i : i + 1, :] = jnp.sum(picked, axis=0, keepdims=True)
+        tau_copy(s).start()
+
+    run(interact, near_first, near_count, whole_cols, 4)
+    run(finish, last_first, last_count, whole_cols, 4)
 
     speed_copy().wait_recv()
     rates[0:1, 0:nf] = speed_far[...].reshape(1, nf)
@@ -479,7 +544,8 @@
             if flag:
                 ahead = jnp.logical_or(ahead, eight[:, 0:8] == i)
         cols_far[here, :] = jnp.where(ahead, left[here], right[here])
-    raw_copy().wait_recv()
+    raw_copy(True).wait_recv()
+    raw_copy(False).wait_recv()
 
     for u in range(far_chunks):
         def halo(r, j):
@@ -490,24 +556,41 @@
             return edge_far[pair * u + 8 * j : pair * u + 8 * j + 8, :]
 
         gain = [gains_far[2 * u + i : 2 * u + i + 1, :] for i in range(2)]
-        propagate(far_first + u, outer, gain, halo, ())
+        propagate(far_first + u, outer, gain, halo, range(rows), {})
 
     late = (chunks - far_chunks - 1) * other + fi
-    lax.fori_loop(late, late + 2, interact, 0)
-    late = (chunks - 2 * far_chunks) * other + fi * far_chunks
-    lax.fori_loop(late, late + 2, finish, 0)
+    run(interact, late, 2, whole_cols, 2)
+    energy_copy().wait()
+    loss = time_step * dissip[...] * ((energy[0:rows, :] + energy_got[0:rows, :]) / nbins)
 
     def settle(t, carry):
-        at = pl.multiple_of((t + first) * pitch, 8)
+        at = pl.multiple_of((t + last_first) * pitch, 8)
         for r in range(rows):
-            spot = pl.ds(t * (pair * rows) + r, pair, stride=rows)
-            e = mf[pl.ds(at, pair), r * LANES : (r + 1) * LANES]
+            spot = pl.ds((t + last_first - first) * (pair * rows) + r, pair, stride=rows)
+            e = mf[pl.ds(at, pair), columns(r)]
             result[spot, :] = result[spot, :] - e * loss[r : r + 1, :]
         return carry
 
-    lax.fori_loop(0, own_chunks, settle, 0)
-
-    raw_copy().wait_send()
+    lax.fori_loop(0, last_count, settle, 0)
+
+    late = (chunks - 2 * far_chunks) * other + fi * far_chunks
+    run(functools.partial(finish, loss=loss), late, 2, whole_cols, 2)
+
+    st = tau_own[...]
+    for s in range(len(group)):
+        tau_copy(s).wait()
+        st = st + taus[s]
+    wide = sum(
+        jnp.dot(term, spread_out[...], preferred_element_type=F32) for term in thirds(st)
+    )
+    place = lax.broadcasted_iota(jnp.int32, (all_rows, share), 1) & (all_rows - 1)
+    own_row = place == lax.broadcasted_iota(jnp.int32, (all_rows, share), 0)
+    for i in range(2):
+        picked = jnp.where(own_row, wide[i * all_rows : (i + 1) * all_rows], 0.0)
+        stress[i : i + 1, :] = jnp.sum(picked, axis=0, keepdims=True)
+
+    raw_copy(True).wait_send()
+    raw_copy(False).wait_send()
     speed_copy().wait_send()
     for flag in (True, False):
         lon_copy(flag).wait_send()
@@ -567,8 +650,6 @@
 
     packed = round_up(nf * half, 8)
     far_lat = EDGE * half
-    peers = n_lat * n_freq - 1
-    small = 8 + 2 * all_rows
     share = (width // n_freq) * all_rows
     span = round_up(max(nbins, (chunks + 2) * pitch), LANES)
     reach = round_up(3 * pitch, LANES)
@@ -630,11 +711,14 @@
             VMEM((8, width), F32),
             VMEM((8, width), F32),
             VMEM((pair, 8), F32),
-            VMEM((small, width), F32),
-            VMEM((peers, small, width), F32),
-            dma, dma((len(smalls),)),
-            dma((2,)), dma((2,)), dma((4,)), dma((4,)), dma((4,)), dma((4,)),
-            dma((peers,)), dma((peers,)),
+            VMEM((width, share), BF16),
+            VMEM((8, width), F32),
+            VMEM((8, width), F32),
+            VMEM((2 * all_rows, width), F32),
+            VMEM((n_lat * n_freq - 1, 2 * all_rows, width), F32),
+            dma((nf // 2,)), dma((len(smalls),)), pltpu.SemaphoreType.REGULAR,
+            dma((3,)), dma((3,)), dma((4,)), dma((4,)), dma((4,)), dma((4,)),
+            dma((1,)), dma((1,)), dma((n_lat * n_freq - 1,)), dma((n_lat * n_freq - 1,)),
         ],
         compiler_params=pltpu.CompilerParams(
             collective_id=0, has_side_effects=True, vmem_limit_bytes=32 << 20

time: 20.3 us -> 17 us (0.84)
  Pallas kernels: 19.5 us -> 16.2 us
    pallas_call x1, Pallas kernels: 18.4 us -> 15.1 us  [local(): pl.pallas_call(functools.partial(wave_kernel, sizes, (cosines, sines)), o...]
where the time goes in v2:
time: 17 us; the launch traced here: 16.9 us
  Pallas kernels  16.2 us (95%)
  between operations  0.64 us (4%)
    pallas_call x1, Pallas kernels, local(): pl.pallas_call(functools.partial(wave_kernel, sizes, (cosines, sines)), o...  15.1 us
    pallas_call x1, Pallas kernels, local(): pl.pallas_call(write_kernel, out_shape=(jax.ShapeDtypeStruct((band * rows...  1.1 us

profile of v2, /device:TPU:0, one launch (start us, length us, event | category | flops | bytes accessed | tf_op | source)
XLA Modules:
  0.0 16.9 jit_solution(5831263515149673673)
XLA Ops:
  0.6 15.1 %shard_map.122 = (f32[2592,128]{1,0:T(8,128)S(1)}, f32[2,512]{1,0:T(2,128)S(1)}) custom-call(f32[2592,128]{1,0:T(8,128)} %bitcast.3, f32[18]{0:T(128)} %refs_0_.1, f32[8,128]{1,0:T(8,128)} %constant.2.clone.refs_1_, f32[1296]{0:T(1024)} %refs_2_.1, f32[1296]{0:T(1024)} %refs_3_.1, f32[2,1296]{1,0:T(2,128)} %refs_4_.1, s32[2,1296]{1,0:T(2,128)} %refs_5_.1, ...), custom_call_target="tpu_custom_call" | custom-call | tf_op jit(solution)/shard_map/pallas_call | solution.py:672
  15.8 1.1 %shard_map.123 = (f32[2592,128]{1,0:T(8,128)}, f32[2,512]{1,0:T(2,128)}) custom-call(f32[2592,128]{1,0:T(8,128)S(1)} %get-tuple-element.6.result, f32[2,512]{1,0:T(2,128)S(1)} %get-tuple-element.7.stress), custom_call_target="tpu_custom_call" | custom-call | tf_op jit(solution)/shard_map/pallas_call | solution.py:732

commit v3 on v2

--- a/solution.py
+++ b/solution.py
@@ -36,16 +36,50 @@
     return high, low, rest.astype(BF16)
 
 
+def layout(rows):
+    inner, rim_rows = list(range(1, rows - 1)), [0, rows - 1]
+    slot = {r: i for i, r in enumerate(inner + rim_rows)}
+
+    def columns(r):
+        return slice(slot[r] * LANES, slot[r] * LANES + LANES)
+
+    whole = slice(0, rows * LANES)
+    split_at = len(inner) * LANES
+    return inner, rim_rows, columns, (whole, slice(0, split_at), slice(split_at, rows * LANES))
+
+
+def finish_chunk(c, first, cs, shape, refs, result, growth, stay):
+    nd, rows = shape
+    put, th, tl, shapes, mf = refs
+    pair = 2 * nd
+    pitch = round_up(pair, 16)
+    window = 3 * pitch
+    columns = layout(rows)[2]
+    at = pl.multiple_of(c * pitch, 16)
+    lhs = put[pl.ds(at, pitch), :window]
+    back = jnp.dot(lhs, th[pl.ds(at, window), cs], preferred_element_type=F32)
+    back = back + jnp.dot(lhs, tl[pl.ds(at, window), cs], preferred_element_type=F32)
+    profile = shapes[pl.ds(at, pair), :]
+    to = (c - first) * (pair * rows)
+    for r in range(rows):
+        here = columns(r)
+        if here.start < cs.start or here.stop > cs.stop:
+            continue
+        e = mf[pl.ds(at, pair), here]
+        gain = back[:pair, here.start - cs.start : here.stop - cs.start]
+        result[pl.ds(to + r, pair, stride=rows), :] = e * (stay(r) + profile * growth(r)) + gain
+
+
 def wave_kernel(sizes, angles, spectrum, *refs):
     sources, refs = refs[:10], refs[10:]
-    result, stress, *refs = refs
+    result, mf, th, tl, put, shapes, factors, stress, spread_out, *refs = refs
     inputs, refs = refs[:10], refs[10:]
     speed, waves, profile, coef, momentum, quad, mask, wind, dissip, cells = inputs
     (
-        x, mf, mh, ml, th, tl, pick, put, table, rates, cols, lines, coefs, shapes, weight0, weight1,
+        x, mh, ml, pick, table, rates, cols, lines, coefs, weight0, weight1,
         gains, gains_far, speed_far, pack_up, pack_down, got_up, got_down, edge, edge_far,
-        lon_pack, got_left, got_right, lon_far, far_left, far_right, cols_far, spread_out, energy, energy_got, tau_own, taus,
-        load_sem, small_sem, ready_sem, raw_send, raw_recv, lat_send, lat_recv, lon_send, lon_recv,
+        lon_pack, got_left, got_right, lon_far, far_left, far_right, cols_far, energy, energy_got, tau_own, taus,
+        load_sem, small_sem, lat_ready, diag_ready, lon_ready, raw_send, raw_recv, lat_send, lat_recv, lon_send, lon_recv,
         sum_send, sum_recv, tau_send, tau_recv,
     ) = refs
     n_lat, n_lon, n_freq, nf, nd, rows, nbins = sizes
@@ -93,16 +127,46 @@
         dl, df = divmod(s, n_freq)
         group.append({"lat": lax.rem(li + dl, n_lat), "freq": lax.rem(fi + df, n_freq)})
     barrier = pltpu.get_barrier_semaphore()
-    beside = [{"lon": east}, {"lon": west}]
-    beside += [{"lon": east, "freq": other}, {"lon": west, "freq": other}]
-    odd = lax.rem(lo, 2)
-    for peer in group:
-        pl.semaphore_signal(barrier, inc=1, device_id=peer, device_id_type=MESH)
-
-    @pl.when(odd == 0)
-    def _():
-        for peer in beside:
-            pl.semaphore_signal(barrier, inc=1, device_id=peer, device_id_type=MESH)
+    last = n_lon - 1
+    higher = [li + dl < n_lat for dl in range(1, n_lat)]
+    lat_peer = [
+        [{"lat": lax.rem(li + dl, n_lat), "freq": f} for f in range(n_freq)] for dl in range(1, n_lat)
+    ]
+    beside = {
+        side: [{"lon": side_at, "freq": f} for f in range(n_freq)]
+        for side, side_at in (("east", east), ("west", west))
+    }
+
+    def signal(semaphore, peers):
+        for peer in peers:
+            pl.semaphore_signal(semaphore, inc=1, device_id=peer, device_id_type=MESH)
+
+    def signal_if(condition, semaphore, peers):
+        @pl.when(condition)
+        def _():
+            signal(semaphore, peers)
+
+    signal(barrier, [{"freq": other}])
+    for up, (in_first, in_second) in zip(higher, lat_peer):
+        signal_if(jnp.logical_or(fi == 0, up), barrier, [in_first])
+        signal_if(up, barrier, [in_second])
+    signal_if(lo < last, barrier, beside["east"])
+    signal_if(lo == 0, barrier, beside["west"])
+    at_start, at_end = lax.div(last - lo, last), lax.div(lo, last)
+    greeted = 1 + other * (n_lat - 1 + li) + fi * (2 * li) + 2 * (1 - at_start) + 2 * at_end
+    answers_lat = n_lat - 1 - li
+    answers_lon = 2 * (1 - at_end) + 2 * at_start
+
+    def enter():
+        pl.semaphore_wait(barrier, greeted)
+        speed_copy().start()
+        raw_copy(True).start()
+        for up, (in_first, in_second) in zip(higher, lat_peer):
+            signal_if(jnp.logical_and(fi == 1, jnp.logical_not(up)), lat_ready, [in_second])
+            signal_if(jnp.logical_and(fi == 1, jnp.logical_not(up)), diag_ready, [in_first])
+            signal_if(jnp.logical_and(fi == 0, jnp.logical_not(up)), diag_ready, [in_second])
+        signal_if(lo > 0, lon_ready, beside["west"])
+        signal_if(lo == last, lon_ready, beside["east"])
 
     packed = pack_up.shape[0]
     far_lat = EDGE * half
@@ -192,14 +256,20 @@
     forward = [signs(cosines, j) for j in range(groups)]
     southern = [[(8 * j + i) % nd < half for i in range(8)] for j in range(groups)]
 
+    @pl.when(fi == 1)
+    def _():
+        enter()
+
     pack_up[pl.ds(packed - 8, 8), :] = jnp.zeros((8, LANES), F32)
     pack_down[pl.ds(packed - 8, 8), :] = jnp.zeros((8, LANES), F32)
     sums = [jnp.zeros((8, LANES), F32) for _ in range(groups)]
     for i, copy in enumerate(loads):
         if i == len(loads) - 1:
-            pl.semaphore_wait(barrier, len(group) + odd * len(beside))
-            speed_copy().start()
-            raw_copy(True).start()
+
+            @pl.when(fi == 0)
+            def _():
+                enter()
+
         copy.wait()
         for f in range(2 * step * i, 2 * step * (i + 1)):
             at = half * places[f]
@@ -231,31 +301,39 @@
     turned = pltpu.roll(whole, lax.rem(LANES - begin, LANES), 1).T
     lon_far[...] = turned[0:8, :]
 
-    @pl.when(up_ok)
-    def _():
-        lat_copy(True).start()
-
-    @pl.when(down_ok)
-    def _():
-        lat_copy(False).start()
-
-    @pl.when(up_ok)
-    def _():
-        lat_far_copy(True).start()
-
-    @pl.when(down_ok)
-    def _():
-        lat_far_copy(False).start()
-
-    raw_copy(False).start()
-
-    @pl.when(odd == 1)
-    def _():
-        for peer in beside:
-            pl.semaphore_signal(ready_sem, inc=1, device_id=peer, device_id_type=MESH)
+    def send_columns(answered):
+        if answered:
+            pl.semaphore_wait(lon_ready, answers_lon)
         for to_east in (True, False):
             lon_copy(to_east).start()
             lon_far_copy(to_east).start()
+
+    @pl.when(lo == last)
+    def _():
+        send_columns(False)
+
+    @pl.when(jnp.logical_and(fi == 1, up_ok))
+    def _():
+        pl.semaphore_wait(lat_ready, answers_lat)
+
+    @pl.when(up_ok)
+    def _():
+        lat_copy(True).start()
+
+    @pl.when(down_ok)
+    def _():
+        lat_copy(False).start()
+
+    @pl.when(up_ok)
+    def _():
+        pl.semaphore_wait(diag_ready, answers_lat)
+        lat_far_copy(True).start()
+
+    @pl.when(down_ok)
+    def _():
+        lat_far_copy(False).start()
+
+    raw_copy(False).start()
 
     for copy in small:
         copy.wait()
@@ -291,15 +369,9 @@
     table[pl.ds(0, pair), :] = jnp.broadcast_to(turned[0:pair, 0:1], (pair, LANES))
     table[pl.ds(pair, pair), :] = jnp.broadcast_to(turned[0:pair, 1:2], (pair, LANES))
 
-    def send_columns():
-        pl.semaphore_wait(ready_sem, len(beside))
-        for to_east in (True, False):
-            lon_copy(to_east).start()
-            lon_far_copy(to_east).start()
-
-    @pl.when(jnp.logical_and(odd == 0, lo > 0))
-    def _():
-        send_columns()
+    @pl.when(jnp.logical_and(lo > 0, lo < last))
+    def _():
+        send_columns(True)
 
     @pl.when(jnp.logical_not(down_ok))
     def _():
@@ -344,17 +416,11 @@
 
     @pl.when(lo == 0)
     def _():
-        send_columns()
+        send_columns(True)
 
     sea = mask[...].astype(F32)
 
-    inner, rim_rows = list(range(1, rows - 1)), [0, rows - 1]
-    slot = {r: i for i, r in enumerate(inner + rim_rows)}
-    whole_cols = slice(0, rows * LANES)
-    inner_cols, rim_cols = slice(0, len(inner) * LANES), slice(len(inner) * LANES, rows * LANES)
-
-    def columns(r):
-        return slice(slot[r] * LANES, slot[r] * LANES + LANES)
+    inner, rim_rows, columns, (whole_cols, inner_cols, rim_cols) = layout(rows)
 
     def upwind(e, j):
         if all(forward[j]):
@@ -420,22 +486,11 @@
         th[pl.ds(to, pitch), cs] = hi
         tl[pl.ds(to, pitch), cs] = lw
 
-    def finish(c, cs, loss=None):
-        at = pl.multiple_of(c * pitch, 16)
-        lhs = put[pl.ds(at, pitch), :window]
-        back = jnp.dot(lhs, th[pl.ds(at, window), cs], preferred_element_type=F32)
-        back = back + jnp.dot(lhs, tl[pl.ds(at, window), cs], preferred_element_type=F32)
-        shape = shapes[pl.ds(at, pair), :]
-        to = (c - first) * (pair * rows)
-        for r in range(rows):
-            here = columns(r)
-            if here.start < cs.start or here.stop > cs.stop:
-                continue
-            e = mf[pl.ds(at, pair), here]
-            stay = 1.0 if loss is None else 1.0 - loss[r : r + 1, :]
-            growth = stay + shape * (time_step * wind[r : r + 1, :])
-            gain = back[:pair, here.start - cs.start : here.stop - cs.start]
-            result[pl.ds(to + r, pair, stride=rows), :] = e * growth + gain
+    def finish(c, cs):
+        finish_chunk(
+            c, first, cs, (nd, rows), (put, th, tl, shapes, mf), result,
+            lambda r: time_step * wind[r : r + 1, :], lambda r: 1.0,
+        )
 
     def run(what, begin, count, cs, at_once):
         def body(t, carry):
@@ -561,25 +616,74 @@
     late = (chunks - far_chunks - 1) * other + fi
     run(interact, late, 2, whole_cols, 2)
     energy_copy().wait()
-    loss = time_step * dissip[...] * ((energy[0:rows, :] + energy_got[0:rows, :]) / nbins)
-
-    def settle(t, carry):
-        at = pl.multiple_of((t + last_first) * pitch, 8)
-        for r in range(rows):
-            spot = pl.ds((t + last_first - first) * (pair * rows) + r, pair, stride=rows)
-            e = mf[pl.ds(at, pair), columns(r)]
-            result[spot, :] = result[spot, :] - e * loss[r : r + 1, :]
-        return carry
-
-    lax.fori_loop(0, last_count, settle, 0)
-
-    late = (chunks - 2 * far_chunks) * other + fi * far_chunks
-    run(functools.partial(finish, loss=loss), late, 2, whole_cols, 2)
+    factors[0:rows, :] = time_step * dissip[...] * ((energy[0:rows, :] + energy_got[0:rows, :]) / nbins)
+    factors[rows : 2 * rows, :] = time_step * wind[...]
 
     st = tau_own[...]
     for s in range(len(group)):
         tau_copy(s).wait()
         st = st + taus[s]
+    stress[...] = st
+
+    raw_copy(True).wait_send()
+    raw_copy(False).wait_send()
+    speed_copy().wait_send()
+    for flag in (True, False):
+        lon_copy(flag).wait_send()
+        lon_far_copy(flag).wait_send()
+
+    @pl.when(up_ok)
+    def _():
+        lat_copy(True).wait_send()
+        lat_far_copy(True).wait_send()
+
+    @pl.when(down_ok)
+    def _():
+        lat_copy(False).wait_send()
+        lat_far_copy(False).wait_send()
+
+
+def write_kernel(
+    sizes, before, mf, th, tl, put, shapes, factors, taus, spread_out, result_out, stress_out,
+    result, stress, sems,
+):
+    n_lat, n_lon, n_freq, nf, nd, rows, nbins = sizes
+    pair = 2 * nd
+    pitch = round_up(pair, 16)
+    own_chunks, far_chunks = nf // 2, EDGE // 2
+    columns, (whole_cols, _, _) = layout(rows)[2:]
+    fi = lax.axis_index("freq")
+    first = far_chunks * fi
+    size = pair * rows
+
+    def out(i):
+        here = pl.ds(pl.multiple_of(lax.rem(i + first, own_chunks) * size, 8), size)
+        return pltpu.make_async_copy(result.at[here], result_out.at[here], sems.at[i])
+
+    def settle(i, carry):
+        t = lax.rem(i + first, own_chunks)
+        at = pl.multiple_of((t + first) * pitch, 8)
+        for r in range(rows):
+            spot = pl.ds(t * size + r, pair, stride=rows)
+            e = mf[pl.ds(at, pair), columns(r)]
+            result[spot, :] = before[spot, :] - e * factors[r : r + 1, :]
+        out(i).start()
+        return carry
+
+    settled = own_chunks - far_chunks
+    lax.fori_loop(0, settled, settle, 0)
+    for i in range(settled, own_chunks):
+        finish_chunk(
+            lax.rem(i + first, own_chunks) + first, first, whole_cols, (nd, rows),
+            (put, th, tl, shapes, mf), result,
+            lambda r: factors[rows + r : rows + r + 1, :], lambda r: 1.0 - factors[r : r + 1, :],
+        )
+    for i in range(settled, own_chunks):
+        out(i).start()
+
+    all_rows = n_lat * rows
+    share = (LANES // n_freq) * all_rows
+    st = taus[...]
     wide = sum(
         jnp.dot(term, spread_out[...], preferred_element_type=F32) for term in thirds(st)
     )
@@ -588,36 +692,15 @@
     for i in range(2):
         picked = jnp.where(own_row, wide[i * all_rows : (i + 1) * all_rows], 0.0)
         stress[i : i + 1, :] = jnp.sum(picked, axis=0, keepdims=True)
-
-    raw_copy(True).wait_send()
-    raw_copy(False).wait_send()
-    speed_copy().wait_send()
-    for flag in (True, False):
-        lon_copy(flag).wait_send()
-        lon_far_copy(flag).wait_send()
-
-    @pl.when(up_ok)
-    def _():
-        lat_copy(True).wait_send()
-        lat_far_copy(True).wait_send()
-
-    @pl.when(down_ok)
-    def _():
-        lat_copy(False).wait_send()
-        lat_far_copy(False).wait_send()
-
-
-def write_kernel(result, stress, result_out, stress_out, sems):
-    pieces = sems.shape[0] - 1
-    size = result.shape[0] // pieces
-    copies = [pltpu.make_async_copy(stress, stress_out, sems.at[pieces])]
-    for i in range(pieces):
-        here = pl.ds(size * i, size)
-        copies.append(pltpu.make_async_copy(result.at[here], result_out.at[here], sems.at[i]))
-    for copy in copies:
-        copy.start()
-    for copy in copies:
-        copy.wait()
+    last = pltpu.make_async_copy(stress, stress_out, sems.at[own_chunks])
+    last.start()
+
+    def wait(i, carry):
+        out(i).wait()
+        return carry
+
+    lax.fori_loop(0, own_chunks, wait, 0)
+    last.wait()
 
 
 def local(
@@ -669,29 +752,35 @@
         dissipation,
         ocean_cell,
     )
-    out, ocean = pl.pallas_call(
+    between = [
+        jax.ShapeDtypeStruct(shape, dtype)
+        for shape, dtype in (
+            ((band * rows, width), F32),
+            ((chunks * pitch, rows * width), F32),
+            (((chunks + 2) * pitch, rows * width), BF16),
+            (((chunks + 2) * pitch, rows * width), BF16),
+            ((chunks * pitch, reach), BF16),
+            ((chunks * pitch, width), F32),
+            ((2 * rows, width), F32),
+            ((2 * all_rows, width), F32),
+            ((width, share), BF16),
+        )
+    ]
+    made = pl.pallas_call(
         functools.partial(wave_kernel, sizes, (cosines, sines)),
-        out_shape=(
-            jax.ShapeDtypeStruct((band * rows, width), F32),
-            jax.ShapeDtypeStruct((2, share), F32),
-        ),
+        out_shape=between,
         in_specs=[hbm] * 11,
-        out_specs=(vmem, vmem),
+        out_specs=[vmem] * len(between),
         scratch_shapes=[VMEM(a.shape, a.dtype) for a in smalls]
         + [
             VMEM((chunks * pair * rows, width), F32),
-            VMEM((chunks * pitch, rows * width), F32),
-            VMEM(((chunks + 2) * pitch, rows * width), BF16),
-            VMEM(((chunks + 2) * pitch, rows * width), BF16),
             VMEM(((chunks + 2) * pitch, rows * width), BF16),
             VMEM(((chunks + 2) * pitch, rows * width), BF16),
             VMEM((2 * chunks * pitch, reach), BF16),
-            VMEM((chunks * pitch, reach), BF16),
             VMEM((2 * pair, width), F32),
             VMEM((8, width), F32),
             VMEM((span, 8), F32),
             VMEM((8, span), F32),
-            VMEM((chunks * pitch, width), F32),
             VMEM((chunks * pitch, width), F32),
             VMEM((chunks * pitch, width), F32),
             VMEM((chunks * pitch, width), F32),
@@ -711,12 +800,12 @@
             VMEM((8, width), F32),
             VMEM((8, width), F32),
             VMEM((pair, 8), F32),
-            VMEM((width, share), BF16),
             VMEM((8, width), F32),
             VMEM((8, width), F32),
             VMEM((2 * all_rows, width), F32),
             VMEM((n_lat * n_freq - 1, 2 * all_rows, width), F32),
-            dma((nf // 2,)), dma((len(smalls),)), pltpu.SemaphoreType.REGULAR,
+            dma((nf // 2,)), dma((len(smalls),)),
+            *[pltpu.SemaphoreType.REGULAR] * 3,
             dma((3,)), dma((3,)), dma((4,)), dma((4,)), dma((4,)), dma((4,)),
             dma((1,)), dma((1,)), dma((n_lat * n_freq - 1,)), dma((n_lat * n_freq - 1,)),
         ],
@@ -730,16 +819,18 @@
         ]
     )
     out, ocean = pl.pallas_call(
-        write_kernel,
+        functools.partial(write_kernel, sizes),
         out_shape=(
             jax.ShapeDtypeStruct((band * rows, width), F32),
             jax.ShapeDtypeStruct((2, share), F32),
         ),
-        in_specs=[vmem, vmem],
+        in_specs=[vmem] * len(between),
         out_specs=(hbm, hbm),
-        scratch_shapes=[dma((5,))],
-        compiler_params=pltpu.CompilerParams(vmem_limit_bytes=1 << 20),
-    )(out, ocean)
+        scratch_shapes=[
+            VMEM((band * rows, width), F32), VMEM((2, share), F32), dma((nf // 2 + 1,)),
+        ],
+        compiler_params=pltpu.CompilerParams(vmem_limit_bytes=16 << 20),
+    )(*made)
     return out.reshape(spectrum.shape), ocean.T
 
 

time: 17 us -> 16.6 us (0.976)
  Pallas kernels: 16.2 us -> 15.8 us
    pallas_call x1, Pallas kernels: 15.1 us -> 14.5 us  [local(): pl.pallas_call(functools.partial(wave_kernel, sizes, (cosines, sines)), o...]
    pallas_call x1, Pallas kernels: 1.1 us -> 1.34 us  [local(): pl.pallas_call(functools.partial(write_kernel, sizes), out_shape=(jax.Sha...]
where the time goes in v3:
time: 16.6 us; the launch traced here: 16.5 us
  Pallas kernels  15.8 us (95%)
  between operations  0.64 us (4%)
    pallas_call x1, Pallas kernels, local(): pl.pallas_call(functools.partial(wave_kernel, sizes, (cosines, sines)), o...  14.5 us
    pallas_call x1, Pallas kernels, local(): pl.pallas_call(functools.partial(write_kernel, sizes), out_shape=(jax.Sha...  1.34 us

profile of v3, /device:TPU:0, one launch (start us, length us, event | category | flops | bytes accessed | tf_op | source)
XLA Modules:
  0.0 16.5 jit_solution(17974498384486017908)
XLA Ops:
  0.6 14.5 %shard_map.122 = (f32[2592,128]{1,0:T(8,128)S(1)}, f32[880,512]{1,0:T(8,128)S(1)}, bf16[1040,512]{1,0:T(8,128)(2,1)S(1)}, bf16[1040,512]{1,0:T(8,128)(2,1)S(1)},...) custom-call(f32[2592,128]{1,0:T(8,128)} %bitcast.3, ...), custom_call_target="tpu_custom_call" | custom-call | tf_op jit(solution)/shard_map/pallas_call | solution.py:769
  15.1 1.3 %shard_map.123 = (f32[2592,128]{1,0:T(8,128)}, f32[2,512]{1,0:T(2,128)}) custom-call(f32[2592,128]{1,0:T(8,128)S(1)} %get-tuple-element.13.before, f32[880,512]{1,0:T(8,128)S(1)} %get-tuple-element.14.mf, bf16[1040,512]{1,0:T(8,128)(2,1)S(1)} %get-tuple-element.15.th, bf16[1040,512]{1,0:T(8,128)(2,1)S(1)} %get-tuple-element.16.tl, ...), custom_call_target="tpu_custom_call" | custom-call | tf_op jit(solution)/shard_map/pallas_call | solution.py:821

commit v4 on v3

--- a/solution.py
+++ b/solution.py
@@ -76,7 +76,7 @@
     inputs, refs = refs[:10], refs[10:]
     speed, waves, profile, coef, momentum, quad, mask, wind, dissip, cells = inputs
     (
-        x, mh, ml, pick, table, rates, cols, lines, coefs, weight0, weight1,
+        x, mh, ml, pick, table, rates, cols, lines, coefs, weight0, weight1, rim_weights,
         gains, gains_far, speed_far, pack_up, pack_down, got_up, got_down, edge, edge_far,
         lon_pack, got_left, got_right, lon_far, far_left, far_right, cols_far, energy, energy_got, tau_own, taus,
         load_sem, small_sem, lat_ready, diag_ready, lon_ready, raw_send, raw_recv, lat_send, lat_recv, lon_send, lon_recv,
@@ -339,6 +339,7 @@
         copy.wait()
     rates[...] = jnp.zeros_like(rates)
     rates[0:1, 0:nf] = speed[...].reshape(1, nf)
+    own_rates = rates[...]
     gains[...] = jnp.broadcast_to(
         pltpu.roll(rates[...], EDGE * fi, 1).T[0 : gains.shape[0], 0:1], gains.shape
     )
@@ -429,6 +430,67 @@
             return pltpu.roll(e, LANES - 1, 1)
         at = lane + jnp.where(rows_of(forward[j]), LANES - 1, 1)
         return jnp.take_along_axis(e, at & (LANES - 1), axis=1)
+
+    def rates_of(j, gain):
+        low, high = 8 * j < nd, 8 * j + 8 > nd
+        if low and high:
+            g = jnp.where(eight < nd - 8 * j, gain[0], gain[1])
+        else:
+            g = jnp.broadcast_to(gain[0] if low else gain[1], (8, LANES))
+        return g * table[8 * j : 8 * j + 8, :], g * table[pair + 8 * j : pair + 8 * j + 8, :]
+
+    def rim_lane(j):
+        return lane == choose(forward[j], lambda: 0, lambda: LANES - 1)
+
+    def prepare(c, gain, sums):
+        base = pl.multiple_of(c * (pair * rows), 8)
+        at = pl.multiple_of(c * pitch, 16)
+        zero = jnp.zeros((8, LANES), F32)
+        for j in range(groups):
+            ax, ay = rates_of(j, gain)
+            stay = 1.0 - ax - ay
+            weights = weight0[pl.ds(at + 8 * j, 8), :], weight1[pl.ds(at + 8 * j, 8), :]
+            e = [x[pl.ds(base + 8 * rows * j + r, 8, stride=rows), :] for r in range(rows)]
+            for r in range(rows):
+                nx = jnp.where(rim_lane(j), 0.0, upwind(e[r], j))
+                ny = choose(
+                    southern[j],
+                    lambda: e[r - 1] if r > 0 else zero,
+                    lambda: e[r + 1] if r < rows - 1 else zero,
+                )
+                m = stay * e[r] + ax * nx + ay * ny
+                mf[pl.ds(at + 8 * j, 8), columns(r)] = m
+                for i, v in enumerate((m, m * weights[0], m * weights[1])):
+                    sums[r, i] = sums[r, i] + v
+
+    def complete(c, gain, row_set, keep, outer=None, halo=None):
+        at = pl.multiple_of(c * pitch, 16)
+        store = pl.multiple_of(c * pitch + pitch, 16)
+        held = {}
+        for j in range(groups):
+            ax, ay = rates_of(j, gain)
+            for r in row_set:
+                m = mf[pl.ds(at + 8 * j, 8), columns(r)]
+                if halo:
+                    m = m + ax * jnp.where(rim_lane(j), halo(r, j), 0.0)
+                if not keep:
+                    mf[pl.ds(at + 8 * j, 8), columns(r)] = m
+                    continue
+                from_edge = [
+                    (r == 0 and south) or (r == rows - 1 and not south) for south in southern[j]
+                ]
+                if any(from_edge):
+                    zero = jnp.zeros((8, LANES), F32)
+                    m = m + ay * choose(from_edge, lambda: outer(j), lambda: zero)
+                m = m * sea[r : r + 1, :]
+                mf[pl.ds(at + 8 * j, 8), columns(r)] = m
+                held[j, r] = m
+                if j % 2 == 1 or j == groups - 1:
+                    start = j if j % 2 == 0 else j - 1
+                    both = [held[start, r], held[j, r] if j > start else jnp.zeros_like(m)]
+                    hi, lw = split(jnp.concatenate(both, axis=0))
+                    mh[pl.ds(store + 8 * start, 16), columns(r)] = hi
+                    ml[pl.ds(store + 8 * start, 16), columns(r)] = lw
 
     def propagate(c, outer, gain, halo, row_set, sums):
         base = pl.multiple_of(c * (pair * rows), 8)
@@ -508,8 +570,58 @@
             ref[pl.ds(nd * i, half), :] = got_up[pl.ds(at, half), :]
             ref[pl.ds(nd * i + half, half), :] = got_down[pl.ds(at, half), :]
 
+    names = [(r, i) for r in range(rows) for i in range(3)]
+
+    def prepare_own(t, sums):
+        sums = dict(zip(names, sums))
+        for u in range(step):
+            c = first + t * step + u
+            prepare(c, [gains[pl.ds(2 * c + i, 1), :] for i in range(2)], sums)
+        return tuple(sums[n] for n in names)
+
+    place = lane >> 2 if rows == 4 else lax.div(lane, rows)
+    held_rates = pltpu.roll(own_rates, EDGE * fi, 1)
+    rate = [
+        jnp.take_along_axis(held_rates, jnp.minimum(2 * place + i, LANES - 1), axis=1)[0:1]
+        for i in range(2)
+    ]
+    for j in range(groups):
+        here = slice(8 * j, 8 * j + 8)
+        ax, _ = rates_of(j, rate)
+        heavy = [jnp.zeros((8, LANES), F32) for _ in range(2)]
+        for u in range(own_chunks):
+            at = pl.multiple_of((first + u) * pitch, 8) + 8 * j
+            for i, ref in enumerate((weight0, weight1)):
+                heavy[i] = jnp.where(place == first + u, ref[pl.ds(at, 8), :], heavy[i])
+        rim_weights[0, here, :] = ax
+        rim_weights[1, here, :] = ax * heavy[0]
+        rim_weights[2, here, :] = ax * heavy[1]
+    zeros = tuple(jnp.zeros((8, LANES), F32) for _ in names)
+    sums = dict(zip(names, lax.fori_loop(0, own_chunks // step, prepare_own, zeros)))
+    speed_copy().wait_recv()
+    rates[0:1, 0:nf] = speed_far[...].reshape(1, nf)
+    gains_far[...] = jnp.broadcast_to(
+        pltpu.roll(rates[...], fi * (LANES - (nf - EDGE)), 1).T[0:8, 0:1], gains_far.shape
+    )
+
     lon_copy(True).wait_recv()
     lon_copy(False).wait_recv()
+    ends = []
+    for side, source in ((True, got_left), (False, got_right)):
+        for i in range(3):
+            total = jnp.zeros((8, LANES), F32)
+            for j in range(groups):
+                flags = [flag == side for flag in forward[j]]
+                if any(flags):
+                    here = slice(8 * j, 8 * j + 8)
+                    term = rim_weights[i, here, :] * source[here, :]
+                    total = total + choose(flags, lambda: term, lambda: jnp.zeros_like(term))
+            ends.append(jnp.sum(total, axis=0, keepdims=True))
+    ends = jnp.concatenate(ends + [jnp.zeros((2, LANES), F32)], axis=0)
+    lanes_left = LANES
+    while lanes_left > rows:
+        lanes_left //= 2
+        ends = ends + pltpu.roll(ends, lanes_left, 1)
     for j in range(groups):
         here = slice(8 * j, 8 * j + 8)
         got_left[here, :] = choose(
@@ -518,11 +630,8 @@
             lambda: pltpu.roll(got_right[here, :], LANES - 1, 1),
         )
 
-    def own(row_set):
-        names = [(r, i) for r in row_set for i in range(3)]
-
-        def body(t, sums):
-            sums = dict(zip(names, sums))
+    def own(row_set, columns_too, rows_too):
+        def body(t, carry):
             for u in range(step):
                 c = first + t * step + u
 
@@ -533,17 +642,44 @@
                     return edge[pl.ds(pl.multiple_of((c - first) * pair, 8) + 8 * j, 8), :]
 
                 gain = [gains[pl.ds(2 * c + i, 1), :] for i in range(2)]
-                sums = propagate(c, outer, gain, halo, row_set, sums)
-            return tuple(sums[n] for n in names)
-
-        zeros = tuple(jnp.zeros((8, LANES), F32) for _ in names)
-        return dict(zip(names, lax.fori_loop(0, own_chunks // step, body, zeros)))
+                complete(c, gain, row_set, rows_too, outer, halo if columns_too else None)
+            return carry
+
+        lax.fori_loop(0, own_chunks // step, body, 0)
+
+    def edge_sums(t, sums):
+        sums = list(sums)
+        for u in range(step):
+            c = first + t * step + u
+            at = pl.multiple_of(c * pitch, 16)
+            gain = [gains[pl.ds(2 * c + i, 1), :] for i in range(2)]
+            for j in range(groups):
+                _, ay = rates_of(j, gain)
+                term = ay * edge[pl.ds(pl.multiple_of((c - first) * pair, 8) + 8 * j, 8), :]
+                terms = (
+                    term,
+                    term * weight0[pl.ds(at + 8 * j, 8), :],
+                    term * weight1[pl.ds(at + 8 * j, 8), :],
+                )
+                for side in range(2):
+                    flags = [flag == (side == 0) for flag in southern[j]]
+                    if any(flags):
+                        for i, v in enumerate(terms):
+                            sums[3 * side + i] = sums[3 * side + i] + choose(
+                                flags, lambda: v, lambda: jnp.zeros_like(v)
+                            )
+        return tuple(sums)
 
     near_first = 2 * first - fi
     near_count = chunks - far_chunks - 1
     last_first = 2 * first
     last_count = chunks - 2 * far_chunks
-    sums = own(inner)
+    own(inner, True, True)
+
+    @pl.when(jnp.logical_not(down_ok))
+    def _():
+        own(rim_rows, True, False)
+
     @pl.when(down_ok)
     def _():
         lat_copy(True).wait_recv()
@@ -553,32 +689,48 @@
         lat_copy(False).wait_recv()
 
     receive(edge, far_lat, [places[f] for f in range(nf)])
-    sums.update(own(rim_rows))
+
+    zeros = tuple(jnp.zeros((8, LANES), F32) for _ in range(6))
+    from_rows = lax.fori_loop(0, own_chunks // step, edge_sums, zeros)
+
+    def whole_sum(r, i):
+        total = sums[r, i]
+        if r == 0:
+            total = total + from_rows[i]
+        if r == rows - 1:
+            total = total + from_rows[3 + i]
+        total = jnp.sum(total, axis=0, keepdims=True)
+        start = pltpu.roll(ends, (LANES - r) % LANES, 1)[i : i + 1]
+        stop = pltpu.roll(ends, LANES - 1 - r, 1)[3 + i : 4 + i]
+        total = total + jnp.where(lane[0:1] == 0, start, 0.0)
+        total = total + jnp.where(lane[0:1] == LANES - 1, stop, 0.0)
+        return total * sea[r : r + 1, :]
 
     energy[...] = jnp.zeros((8, LANES), F32)
     ids = (lo * LANES + lax.broadcasted_iota(jnp.int32, (all_rows, LANES), 1)) * all_rows
     ids = ids + lax.broadcasted_iota(jnp.int32, (all_rows, LANES), 0)
     totals = [jnp.zeros((all_rows, LANES), F32) for _ in range(2)]
     for r in range(rows):
-        energy[r : r + 1, :] = jnp.sum(sums[r, 0], axis=0, keepdims=True)
+        energy[r : r + 1, :] = whole_sum(r, 0)
         hit = cells[r : r + 1, :] == ids
         for i in range(2):
-            tau = wind[r : r + 1, :] * jnp.sum(sums[r, 1 + i], axis=0, keepdims=True)
+            tau = wind[r : r + 1, :] * whole_sum(r, 1 + i)
             totals[i] = totals[i] + jnp.where(hit, tau, 0.0)
     for i in range(2):
         tau_own[pl.ds(i * all_rows, all_rows), :] = totals[i]
+    tau_copy(len(group) - 1).start()
     energy_copy().start()
-    for s in range(len(group)):
+    for s in range(len(group) - 1):
         tau_copy(s).start()
 
+
+    @pl.when(down_ok)
+    def _():
+        own(rim_rows, True, False)
+
+    own(rim_rows, False, True)
     run(interact, near_first, near_count, whole_cols, 4)
     run(finish, last_first, last_count, whole_cols, 4)
-
-    speed_copy().wait_recv()
-    rates[0:1, 0:nf] = speed_far[...].reshape(1, nf)
-    gains_far[...] = jnp.broadcast_to(
-        pltpu.roll(rates[...], fi * (LANES - (nf - EDGE)), 1).T[0:8, 0:1], gains_far.shape
-    )
 
     @pl.when(down_ok)
     def _():
@@ -619,12 +771,6 @@
     factors[0:rows, :] = time_step * dissip[...] * ((energy[0:rows, :] + energy_got[0:rows, :]) / nbins)
     factors[rows : 2 * rows, :] = time_step * wind[...]
 
-    st = tau_own[...]
-    for s in range(len(group)):
-        tau_copy(s).wait()
-        st = st + taus[s]
-    stress[...] = st
-
     raw_copy(True).wait_send()
     raw_copy(False).wait_send()
     speed_copy().wait_send()
@@ -641,6 +787,12 @@
     def _():
         lat_copy(False).wait_send()
         lat_far_copy(False).wait_send()
+
+    st = tau_own[...]
+    for s in range(len(group)):
+        tau_copy(s).wait()
+        st = st + taus[s]
+    stress[...] = st
 
 
 def write_kernel(
@@ -784,6 +936,7 @@
             VMEM((chunks * pitch, width), F32),
             VMEM((chunks * pitch, width), F32),
             VMEM((chunks * pitch, width), F32),
+            VMEM((3, pair, width), F32),
             VMEM((round_up(nf + EDGE, 8), width), F32),
             VMEM((8, width), F32),
             VMEM(group_speed.shape, F32),

time: 16.6 us -> 16.3 us (0.982)
  Pallas kernels: 15.8 us -> 15.5 us
    pallas_call x1, Pallas kernels: 14.5 us -> 14.2 us  [local(): pl.pallas_call(functools.partial(wave_kernel, sizes, (cosines, sines)), o...]
where the time goes in v4:
time: 16.3 us; the launch traced here: 16.2 us
  Pallas kernels  15.5 us (95%)
  between operations  0.64 us (4%)
    pallas_call x1, Pallas kernels, local(): pl.pallas_call(functools.partial(wave_kernel, sizes, (cosines, sines)), o...  14.2 us
    pallas_call x1, Pallas kernels, local(): pl.pallas_call(functools.partial(write_kernel, sizes), out_shape=(jax.Sha...  1.34 us

profile of v4, /device:TPU:0, one launch (start us, length us, event | category | flops | bytes accessed | tf_op | source)
XLA Modules:
  0.0 16.2 jit_solution(6314437512365256185)
XLA Ops:
  0.6 14.2 %shard_map.122 = (f32[2592,128]{1,0:T(8,128)S(1)}, f32[880,512]{1,0:T(8,128)S(1)}, bf16[1040,512]{1,0:T(8,128)(2,1)S(1)}, bf16[1040,512]{1,0:T(8,128)(2,1)S(1)},...) custom-call(f32[2592,128]{1,0:T(8,128)} %bitcast.3, ...), custom_call_target="tpu_custom_call" | custom-call | tf_op jit(solution)/shard_map/pallas_call | solution.py:921
  14.8 1.3 %shard_map.123 = (f32[2592,128]{1,0:T(8,128)}, f32[2,512]{1,0:T(2,128)}) custom-call(f32[2592,128]{1,0:T(8,128)S(1)} %get-tuple-element.13.before, f32[880,512]{1,0:T(8,128)S(1)} %get-tuple-element.14.mf, bf16[1040,512]{1,0:T(8,128)(2,1)S(1)} %get-tuple-element.15.th, bf16[1040,512]{1,0:T(8,128)(2,1)S(1)} %get-tuple-element.16.tl, ...), custom_call_target="tpu_custom_call" | custom-call | tf_op jit(solution)/shard_map/pallas_call | solution.py:974

commit v5 on v4

--- a/solution.py
+++ b/solution.py
@@ -729,8 +729,8 @@
         own(rim_rows, True, False)
 
     own(rim_rows, False, True)
-    run(interact, near_first, near_count, whole_cols, 4)
-    run(finish, last_first, last_count, whole_cols, 4)
+    run(interact, near_first, near_count, whole_cols, 8)
+    run(finish, last_first, last_count, whole_cols, 7)
 
     @pl.when(down_ok)
     def _():

time: 16.3 us -> 16.2 us (level)
  no operation moved by 1% of the time
where the time goes in v5:
time: 16.2 us; the launch traced here: 16 us
  Pallas kernels  15.4 us (95%)
  between operations  0.64 us (4%)
    pallas_call x1, Pallas kernels, local(): pl.pallas_call(functools.partial(wave_kernel, sizes, (cosines, sines)), o...  14.1 us
    pallas_call x1, Pallas kernels, local(): pl.pallas_call(functools.partial(write_kernel, sizes), out_shape=(jax.Sha...  1.34 us

profile of v5, /device:TPU:0, one launch (start us, length us, event | category | flops | bytes accessed | tf_op | source)
XLA Modules:
  0.0 16.0 jit_solution(15648180030624662696)
XLA Ops:
  0.6 14.1 %shard_map.122 = (f32[2592,128]{1,0:T(8,128)S(1)}, f32[880,512]{1,0:T(8,128)S(1)}, bf16[1040,512]{1,0:T(8,128)(2,1)S(1)}, bf16[1040,512]{1,0:T(8,128)(2,1)S(1)},...) custom-call(f32[2592,128]{1,0:T(8,128)} %bitcast.3, ...), custom_call_target="tpu_custom_call" | custom-call | tf_op jit(solution)/shard_map/pallas_call | solution.py:921
  14.7 1.3 %shard_map.123 = (f32[2592,128]{1,0:T(8,128)}, f32[2,512]{1,0:T(2,128)}) custom-call(f32[2592,128]{1,0:T(8,128)S(1)} %get-tuple-element.13.before, f32[880,512]{1,0:T(8,128)S(1)} %get-tuple-element.14.mf, bf16[1040,512]{1,0:T(8,128)(2,1)S(1)} %get-tuple-element.15.th, bf16[1040,512]{1,0:T(8,128)(2,1)S(1)} %get-tuple-element.16.tl, ...), custom_call_target="tpu_custom_call" | custom-call | tf_op jit(solution)/shard_map/pallas_call | solution.py:974

commit v6 on v5

--- a/solution.py
+++ b/solution.py
@@ -631,9 +631,11 @@
         )
 
     def own(row_set, columns_too, rows_too):
+        at_once = step if columns_too else own_chunks
+
         def body(t, carry):
-            for u in range(step):
-                c = first + t * step + u
+            for u in range(at_once):
+                c = first + t * at_once + u
 
                 def halo(r, j):
                     return pltpu.roll(got_left[8 * j : 8 * j + 8, :], LANES - (c * rows + r), 1)
@@ -645,7 +647,7 @@
                 complete(c, gain, row_set, rows_too, outer, halo if columns_too else None)
             return carry
 
-        lax.fori_loop(0, own_chunks // step, body, 0)
+        lax.fori_loop(0, own_chunks // at_once, body, 0)
 
     def edge_sums(t, sums):
         sums = list(sums)

time: 16.2 us -> 16.1 us (level)
  no operation moved by 1% of the time
where the time goes in v6:
time: 16.1 us; the launch traced here: 15.9 us
  Pallas kernels  15.3 us (95%)
  between operations  0.64 us (4%)
    pallas_call x1, Pallas kernels, local(): pl.pallas_call(functools.partial(wave_kernel, sizes, (cosines, sines)), o...  13.9 us
    pallas_call x1, Pallas kernels, local(): pl.pallas_call(functools.partial(write_kernel, sizes), out_shape=(jax.Sha...  1.34 us

profile of v6, /device:TPU:0, one launch (start us, length us, event | category | flops | bytes accessed | tf_op | source)
XLA Modules:
  0.0 15.9 jit_solution(9902047213012466739)
XLA Ops:
  0.6 13.9 %shard_map.122 = (f32[2592,128]{1,0:T(8,128)S(1)}, f32[880,512]{1,0:T(8,128)S(1)}, bf16[1040,512]{1,0:T(8,128)(2,1)S(1)}, bf16[1040,512]{1,0:T(8,128)(2,1)S(1)},...) custom-call(f32[2592,128]{1,0:T(8,128)} %bitcast.3, ...), custom_call_target="tpu_custom_call" | custom-call | tf_op jit(solution)/shard_map/pallas_call | solution.py:923
  14.6 1.3 %shard_map.123 = (f32[2592,128]{1,0:T(8,128)}, f32[2,512]{1,0:T(2,128)}) custom-call(f32[2592,128]{1,0:T(8,128)S(1)} %get-tuple-element.13.before, f32[880,512]{1,0:T(8,128)S(1)} %get-tuple-element.14.mf, bf16[1040,512]{1,0:T(8,128)(2,1)S(1)} %get-tuple-element.15.th, bf16[1040,512]{1,0:T(8,128)(2,1)S(1)} %get-tuple-element.16.tl, ...), custom_call_target="tpu_custom_call" | custom-call | tf_op jit(solution)/shard_map/pallas_call | solution.py:976
